TPU v7x, 128 devices: a whole 4x4x4 slice. The times are simulated.
128 devices in a mesh: gy: 16 (over z, x), gz: 8 (over y, core).
Axes of the slice: x: 4, y: 4, z: 4, core: 2. Of those that a mesh axis runs over, the one named last changes fastest.
Arguments:
- fraction: float32 [128, 128, 1024], P('gz', 'gy'), may hold values from 0 to 1
- velocity_x: float32 [128, 128, 1024], P('gz', 'gy'), may hold values from -9 to 9
- velocity_y: float32 [128, 128, 1024], P('gz', 'gy'), may hold values from -9 to 9
- velocity_z: float32 [128, 128, 1024], P('gz', 'gy'), may hold values from -9 to 9
Outputs:
- advected: float32 [128, 128, 1024], P('gz', 'gy')
- time_step: float32 [], replicated
All inputs are finite; a program needn't handle non-finite values. Where the computation divides by a largest or mean magnitude, that divisor is 1e-20 or more.
Results may differ from a plain program's by a relative error of at most 0.0003.
Values sent between devices are 32-bit elements; how exact they have to be, the bound alone decides.
A program may use at most 64 MiB of HBM per device.

v0:
```python
import functools

import jax
import jax.numpy as jnp
from jax import lax
from jax.experimental import pallas as pl
from jax.experimental.pallas import tpu as pltpu
from jax.sharding import PartitionSpec as P

NEWTON = 5
LANES = 128
GROUP = 8

tilt_floor = 0.1
courant = 0.45
epsilon = 1e-06
tiny = 1e-30

MESH = pl.DeviceIdType.MESH
SIDES = [(a, b) for a in (-1, 0, 1) for b in (-1, 0, 1) if (a, b) != (0, 0)]


def lane_of(value):
    return lax.broadcasted_iota(jnp.int32, value.shape, value.ndim - 1)


def x_next(value):
    turned = pltpu.roll(value, LANES - 1, value.ndim - 1)
    carried = pltpu.roll(turned, value.shape[-2] - 1, value.ndim - 2)
    return jnp.where(lane_of(value) == LANES - 1, carried, turned)


def x_prev(value):
    turned = pltpu.roll(value, 1, value.ndim - 1)
    carried = pltpu.roll(turned, 1, value.ndim - 2)
    return jnp.where(lane_of(value) == 0, carried, turned)


def solve_offset(g, tilt_a, tilt_b, tilt_d):
    volume = jnp.clip(g, 0.0, 1.0)
    lesser = jnp.minimum(volume, 1.0 - volume)
    low = jnp.minimum(tilt_a, tilt_b)
    high = jnp.maximum(tilt_a, tilt_b)
    n1 = jnp.minimum(low, tilt_d)
    middle = jnp.maximum(low, tilt_d)
    n2 = jnp.minimum(middle, high)
    n3 = jnp.maximum(middle, high)
    summed = tilt_a + tilt_b + tilt_d
    inverse = 1.0 / jnp.maximum(n1, tiny)
    third = inverse * (1.0 / 3.0)
    product = n2 * n3
    target = 2.0 * product * lesser
    gap = jnp.maximum(n1 + n2 - n3, 0.0)
    rate = 2.0 * n2 - 0.5 * gap * (gap * inverse)
    offset = 0.5 * summed - (product - target) / rate
    for repeat in range(NEWTON - 1):
        p1 = jnp.minimum(offset, n1)
        q1 = offset - p1
        m2 = jnp.maximum(offset - n2, 0.0)
        p2 = jnp.minimum(m2, n1)
        q2 = m2 - p2
        p3 = jnp.minimum(jnp.maximum(offset - n3, 0.0), n1)
        s1, s2, s3 = p1 * p1, p2 * p2, p3 * p3
        squares = s1 - s2 - s3
        cubes = s1 * p1 - s2 * p2 - s3 * p3
        q = q1 - q2
        rate = squares * inverse + (q + q)
        volume_part = cubes * third + q * (q1 + q2 + n1)
        offset = offset - (volume_part - target) / rate
    return jnp.where(volume > 0.5, summed - offset, offset)


def face_flux(cross, offset, tilt_a, tilt_b, slope):
    turn = slope * cross
    height = jnp.abs(turn)
    reach = offset - jnp.where(turn > 0, 0.0, jnp.abs(slope) - height)

    def parts(value):
        inside = jnp.maximum(value, 0.0)
        p = jnp.minimum(inside, height)
        q = inside - p
        return p * p * p, q * (q + height)

    reach_a = reach - tilt_a
    p0, q0 = parts(reach)
    p1, q1 = parts(reach_a)
    p2, q2 = parts(reach - tilt_b)
    p3, q3 = parts(reach_a - tilt_b)
    cubes = (p0 - p1) - (p2 - p3)
    wholes = (q0 - q1) - (q2 - q3)
    combo = cubes * ((1.0 / 3.0) / jnp.maximum(height, tiny)) + wholes
    return cross * combo / (2.0 * tilt_a * tilt_b)


def kernel(
    n_gy, n_gz, f_hbm, vx_hbm, vy_hbm, vz_hbm, out_ref, dt_ref,
    f_ref, vx_ref, vy_ref, vz_ref, load_sem,
    g0, g1, g2, sx, dx, off, ta, tb, sd, vx, vy, vz, fy, fz,
    fy_in, fz_in, part_y, part_z,
    halo_send, halo_recv, vel_send, vel_recv, flux_send, flux_recv,
    py_send, py_recv, pz_send, pz_recv,
):
    Z = f_ref.shape[0]
    T = sx.shape[2]
    Y = f_ref.shape[1] // T
    loads = []
    for i, (source, target) in enumerate(
        ((f_hbm, f_ref), (vx_hbm, vx_ref), (vy_hbm, vy_ref), (vz_hbm, vz_ref))
    ):
        loads.append(pltpu.make_async_copy(source, target, load_sem.at[i]))
        loads[-1].start()
    my = lax.axis_index("gy")
    mz = lax.axis_index("gz")

    def at(dz, dy):
        return {
            "gy": lax.rem(my + dy + n_gy, n_gy),
            "gz": lax.rem(mz + dz + n_gz, n_gz),
        }

    barrier = pltpu.get_barrier_semaphore()
    greeted = [(0, i) for i in range(1, n_gy)] + [(i, 0) for i in range(1, n_gz)]
    greeted += [(a, b) for a in (-1, 1) for b in (-1, 1)]
    for dz, dy in greeted:
        pl.semaphore_signal(barrier, inc=1, device_id=at(dz, dy), device_id_type=MESH)

    def rows_of(ref, z, y):
        return ref[z, pl.ds(y, T, stride=Y), :]

    def gather(low, high, body, carry):
        count = high - low
        grouped = max(u for u in range(1, GROUP + 1) if count % u == 0)

        def step(i, carry):
            for u in range(grouped):
                carry = body(low + i * grouped + u, carry)
            return carry
        return lax.fori_loop(0, count // grouped, step, carry)

    def loop(low, high, body):
        def step(i, carry):
            body(i)
            return carry
        gather(low, high, step, 0)

    def span(side, count):
        if side == 0:
            return pl.ds(1, count), pl.ds(1, count)
        if side > 0:
            return pl.ds(count, 1), pl.ds(0, 1)
        return pl.ds(1, 1), pl.ds(count + 1, 1)

    def halo_copies(g, which):
        copies = []
        for index, (dz, dy) in enumerate(SIDES):
            src_z, dst_z = span(dz, Z)
            src_y, dst_y = span(dy, Y)
            copies.append(pltpu.make_async_remote_copy(
                src_ref=g.at[src_z, src_y],
                dst_ref=g.at[dst_z, dst_y],
                send_sem=halo_send.at[which, index],
                recv_sem=halo_recv.at[which, index],
                device_id=at(dz, dy),
                device_id_type=MESH,
            ))
        return copies

    def fill(z, total):
        for y in range(Y):
            f = rows_of(f_ref, z, y)
            g0[z + 1, y + 1] = f
            total = total + 4.0 * f * (1.0 - f)
        return total

    loads[0].wait()
    total = gather(0, Z, fill, jnp.zeros((T, LANES), jnp.float32))

    def fill_velocity(z, peak):
        for y in range(Y):
            a = rows_of(vx_ref, z, y)
            b = rows_of(vy_ref, z, y)
            c = rows_of(vz_ref, z, y)
            vx[z, y] = a
            vy[z, y + 1] = b
            vz[z + 1, y] = c
            peak = jnp.maximum(peak, jnp.maximum(jnp.abs(a), jnp.maximum(jnp.abs(b), jnp.abs(c))))
        return peak

    for copy in loads[1:]:
        copy.wait()
    peak = gather(0, Z, fill_velocity, jnp.zeros((T, LANES), jnp.float32))
    first_row = lax.broadcasted_iota(jnp.int32, (T, LANES), 0) == 0

    def joined(sums, peaks):
        sums = jnp.broadcast_to(jnp.sum(sums, axis=0, keepdims=True), (T, LANES))
        peaks = jnp.broadcast_to(jnp.max(peaks, axis=0, keepdims=True), (T, LANES))
        return jnp.where(first_row, sums, peaks)

    def gathered(part, count):
        sums = part[0]
        peaks = part[0]
        for i in range(1, count):
            sums = sums + part[i]
            peaks = jnp.maximum(peaks, part[i])
        return jnp.where(first_row, sums, 0.0), jnp.where(first_row, 0.0, peaks)

    part_y[my] = joined(total, peak)
    pl.semaphore_wait(barrier, len(greeted))
    vel_copies = [
        pltpu.make_async_remote_copy(
            src_ref=vy.at[:, pl.ds(Y, 1)], dst_ref=vy.at[:, pl.ds(0, 1)],
            send_sem=vel_send.at[0], recv_sem=vel_recv.at[0],
            device_id=at(0, 1), device_id_type=MESH,
        ),
        pltpu.make_async_remote_copy(
            src_ref=vz.at[pl.ds(Z, 1)], dst_ref=vz.at[pl.ds(0, 1)],
            send_sem=vel_send.at[1], recv_sem=vel_recv.at[1],
            device_id=at(1, 0), device_id_type=MESH,
        ),
    ]

    def part_copies(part, mine, send, recv, count, along_y):
        copies = []
        for i in range(1, count):
            copies.append(pltpu.make_async_remote_copy(
                src_ref=part.at[mine], dst_ref=part.at[mine],
                send_sem=send.at[i - 1], recv_sem=recv.at[i - 1],
                device_id=at(0, i) if along_y else at(i, 0), device_id_type=MESH,
            ))
        return copies

    y_parts = part_copies(part_y, my, py_send, py_recv, n_gy, True)
    for copy in y_parts:
        copy.start()
    halos0 = halo_copies(g0, 0)
    for copy in halos0:
        copy.start()
    for copy in vel_copies:
        copy.start()

    def smooth_rows(g, z, y, kz, ky):
        value = g[pl.ds(z, kz), pl.ds(y, ky)]
        after, before = x_next(value), x_prev(value)
        sx[pl.ds(z, kz), pl.ds(y, ky)] = before + (value + value) + after
        dx[pl.ds(z, kz), pl.ds(y, ky)] = after - before

    def smooth_inside(g):
        loop(1, Z + 1, lambda z: smooth_rows(g, z, 1, 1, Y))

    def smooth_ghosts(g):
        smooth_rows(g, 0, 0, 1, Y + 2)
        smooth_rows(g, Z + 1, 0, 1, Y + 2)

        def edge(z):
            smooth_rows(g, z, 0, 1, 1)
            smooth_rows(g, z, Y + 1, 1, 1)
        loop(1, Z + 1, edge)

    def smooth_zero(arr):
        mid = arr[1:-1]
        return (arr[:-2] + mid) + (mid + arr[2:])

    def smooth_one(arr):
        mid = arr[:, 1:-1]
        return (arr[:, :-2] + mid) + (mid + arr[:, 2:])

    def plane(g, dim, z, y, kz, ky):
        s = sx[pl.ds(z, kz + 2), pl.ds(y, ky + 2)]
        d = dx[pl.ds(z, kz + 2), pl.ds(y, ky + 2)]
        grad_zero = smooth_one(s[2:] - s[:-2]) * (1.0 / 32.0)
        across = smooth_zero(s)
        grad_one = (across[:, 2:] - across[:, :-2]) * (1.0 / 32.0)
        grad_cells = smooth_one(smooth_zero(d)) * (1.0 / 32.0)
        slopes = (grad_zero, grad_one, grad_cells)
        slope = slopes[dim]
        tilt_a, tilt_b = [jnp.abs(slopes[e]) + tilt_floor for e in range(3) if e != dim]
        value = g[pl.ds(z + 1, kz), pl.ds(y + 1, ky)]
        where = (pl.ds(z, kz), pl.ds(y, ky))
        off[where] = solve_offset(value, tilt_a, tilt_b, jnp.abs(slope))
        ta[where] = tilt_a
        tb[where] = tilt_b
        sd[where] = slope

    half = (Y - 2) // 2
    quarter = Y // 2

    def ends(body, low, high):
        count = high - low

        def step(i):
            z = i * (Z - 1)
            body(z, low, 1, count // 2)
            body(z, low + count // 2, 1, count - count // 2)
        loop(0, 2, step)

    def sides(body, low, high):
        def step(i):
            z = low + 2 * i
            body(z, 0, 2, 1)
            body(z, Y - 1, 2, 1)
        loop(0, (high - low) // 2, step)

    def inside(body, low, high, first=1, last=None):
        count = (Y - 1 if last is None else last) - first

        def step(z):
            if count > 4:
                body(z, first, 1, count // 2)
                body(z, first + count // 2, 1, count - count // 2)
            else:
                body(z, first, 1, count)
        loop(low, high, step)

    def planes(g, dim):
        return lambda z, y, kz, ky: plane(g, dim, z, y, kz, ky)

    smooth_inside(g0)
    inside(planes(g0, 2), 1, Z // 2)
    for copy in y_parts:
        copy.wait()
    part_z[mz] = joined(*gathered(part_y, n_gy))
    z_parts = part_copies(part_z, mz, pz_send, pz_recv, n_gz, False)
    for copy in z_parts:
        copy.start()
    inside(planes(g0, 2), Z // 2, Z - 1)
    for copy in halos0:
        copy.wait()
    smooth_ghosts(g0)
    sides(planes(g0, 2), 0, Z)
    ends(planes(g0, 2), 1, Y - 1)
    for copy in z_parts:
        copy.wait()
    sums, peaks = gathered(part_z, n_gz)
    cells_all = float(Z * Y * T * LANES * n_gy * n_gz)
    share = jnp.broadcast_to(jnp.sum(sums, keepdims=True), (T, LANES)) / cells_all
    umax = jnp.broadcast_to(jnp.max(peaks, keepdims=True), (T, LANES))
    step_value = courant / ((umax + epsilon) * (1.0 + share))
    dt_ref[0, 0] = jnp.max(step_value)
    dt = step_value[None, None]

    def x_update(z, y, kz, ky):
        where = (pl.ds(z, kz), pl.ds(y, ky))
        cross = dt * vx[where]
        upward = cross > 0

        def donor(ref):
            value = ref[where]
            return jnp.where(upward, value, x_next(value))

        flux = face_flux(cross, donor(off), donor(ta), donor(tb), donor(sd))
        value = g0[pl.ds(z + 1, kz), pl.ds(y + 1, ky)]
        g1[pl.ds(z + 1, kz), pl.ds(y + 1, ky)] = (value - flux + x_prev(flux)) / (
            1.0 - cross + x_prev(cross)
        )

    sides(x_update, 0, Z)
    ends(x_update, 1, Y - 1)
    halos1 = halo_copies(g1, 1)
    for copy in halos1:
        copy.start()
    inside(x_update, 1, Z - 1)
    for copy in vel_copies:
        copy.wait()

    smooth_inside(g1)
    inside(planes(g1, 1), 1, Z - 1)
    for copy in halos1:
        copy.wait()
    smooth_ghosts(g1)
    sides(planes(g1, 1), 0, Z)

    def own_flux(velocity, where, at_face, least):
        cross = dt * velocity[at_face]
        cross = jnp.minimum(cross, 0.0) if least else jnp.maximum(cross, 0.0)
        return face_flux(cross, off[where], ta[where], tb[where], sd[where])

    def y_ends(i):
        rows = pl.ds(2 * i, 2)
        first, last = pl.ds(0, 1), pl.ds(Y - 1, 1)
        fy[rows, first] = own_flux(vy, (rows, first), (rows, first), True)
        fy[rows, pl.ds(Y, 1)] = own_flux(vy, (rows, last), (rows, pl.ds(Y, 1)), False)
    loop(0, Z // 2, y_ends)

    def flux_copies(flux, arrived, which, spans, steps):
        copies = []
        for i in range(2):
            copies.append(pltpu.make_async_remote_copy(
                src_ref=flux.at[spans[i]],
                dst_ref=arrived.at[i],
                send_sem=flux_send.at[which, i], recv_sem=flux_recv.at[which, i],
                device_id=at(*steps[i]), device_id_type=MESH,
            ))
        return copies

    every = pl.ds(0, Z)
    y_flux = flux_copies(
        fy, fy_in, 0, [(every, pl.ds(Y, 1)), (every, pl.ds(0, 1))], [(0, 1), (0, -1)]
    )
    for copy in y_flux:
        copy.start()
    ends(planes(g1, 1), 1, Y - 1)

    def between(velocity, at_face, below, above):
        cross = dt * velocity[at_face]
        upward = cross > 0

        def donor(ref):
            return jnp.where(upward, ref[below], ref[above])

        return face_flux(cross, donor(off), donor(ta), donor(tb), donor(sd))

    def y_inside(z):
        rows = pl.ds(z, 1)
        for low, count in ((1, half), (1 + half, Y - 1 - half)):
            fy[rows, pl.ds(low, count)] = between(
                vy, (rows, pl.ds(low, count)), (rows, pl.ds(low - 1, count)), (rows, pl.ds(low, count))
            )
    loop(0, Z, y_inside)

    def y_update(z, y, kz, ky):
        rows = pl.ds(z, kz)
        low, high = pl.ds(y, ky), pl.ds(y + 1, ky)
        at_cells = (pl.ds(z + 1, kz), pl.ds(y + 1, ky))
        g2[at_cells] = (g1[at_cells] - fy[rows, high] + fy[rows, low]) / (
            1.0 - dt * vy[rows, high] + dt * vy[rows, low]
        )

    inside(y_update, 0, Z)
    loop(1, Z + 1, lambda z: smooth_rows(g2, z, 2, 1, Y - 2))
    inside(planes(g2, 0), 1, Z - 1, 2, Y - 2)
    for copy in y_flux:
        copy.wait()

    def y_merge(i):
        rows = pl.ds(4 * i, 4)
        fy[rows, pl.ds(0, 1)] = fy[rows, pl.ds(0, 1)] + fy_in[0, rows]
        fy[rows, pl.ds(Y, 1)] = fy[rows, pl.ds(Y, 1)] + fy_in[1, rows]
    loop(0, Z // 4, y_merge)
    sides(y_update, 0, Z)
    halos2 = halo_copies(g2, 2)
    for copy in halos2:
        copy.start()

    def smooth_sides(z):
        smooth_rows(g2, z, 1, 1, 1)
        smooth_rows(g2, z, Y, 1, 1)
    loop(1, Z + 1, smooth_sides)

    def near_sides(i):
        z = 1 + 2 * i
        plane(g2, 0, z, 1, 2, 1)
        plane(g2, 0, z, Y - 2, 2, 1)
    loop(0, (Z - 2) // 2, near_sides)
    for copy in halos2:
        copy.wait()
    smooth_ghosts(g2)
    ends(planes(g2, 0), 0, Y)

    def z_ends(i):
        cols = pl.ds(2 * i, 2)
        first, last = pl.ds(0, 1), pl.ds(Z - 1, 1)
        fz[first, cols] = own_flux(vz, (first, cols), (first, cols), True)
        fz[pl.ds(Z, 1), cols] = own_flux(vz, (last, cols), (pl.ds(Z, 1), cols), False)
    loop(0, Y // 2, z_ends)
    z_flux = flux_copies(fz, fz_in, 1, [(pl.ds(Z, 1),), (pl.ds(0, 1),)], [(1, 0), (-1, 0)])
    for copy in z_flux:
        copy.start()
    sides(planes(g2, 0), 1, Z - 1)

    def z_inside(z):
        face, below = pl.ds(z, 1), pl.ds(z - 1, 1)
        for low, count in ((0, quarter), (quarter, Y - quarter)):
            cols = pl.ds(low, count)
            fz[face, cols] = between(vz, (face, cols), (below, cols), (face, cols))
    loop(1, Z, z_inside)
    for copy in z_flux:
        copy.wait()
    fz[pl.ds(0, 1)] = fz[pl.ds(0, 1)] + fz_in[0]
    fz[pl.ds(Z, 1)] = fz[pl.ds(Z, 1)] + fz_in[1]

    def z_update(z):
        for y in range(Y):
            value = (g2[z + 1, y + 1] - fz[z + 1, y] + fz[z, y]) / (
                1.0 - step_value * vz[z + 1, y] + step_value * vz[z, y]
            )
            out_ref[z, pl.ds(y, T, stride=Y), :] = value
    loop(0, Z, z_update)


def solution(mesh):
    n_gy, n_gz = mesh.shape["gy"], mesh.shape["gz"]

    def shards(*blocks):
        Z, Y, X = blocks[0].shape
        T = X // LANES

        def split(block):
            return block.reshape(Z, Y, T, LANES).transpose(0, 2, 1, 3).reshape(Z, T * Y, LANES)

        def rows(*lead):
            return pltpu.VMEM((*lead, T, LANES), jnp.float32)

        dma = pltpu.SemaphoreType.DMA
        padded = rows(Z + 2, Y + 2)
        plain = rows(Z, Y)
        field, dt = pl.pallas_call(
            functools.partial(kernel, n_gy, n_gz),
            out_shape=(
                jax.ShapeDtypeStruct((Z, T * Y, LANES), jnp.float32),
                jax.ShapeDtypeStruct((1, 1), jnp.float32),
            ),
            in_specs=[pl.BlockSpec(memory_space=pltpu.HBM)] * 4,
            out_specs=(
                pl.BlockSpec(memory_space=pltpu.VMEM),
                pl.BlockSpec(memory_space=pltpu.SMEM),
            ),
            scratch_shapes=[
                *[pltpu.VMEM((Z, T * Y, LANES), jnp.float32)] * 4, dma((4,)),
                padded, padded, padded, padded, padded,
                plain, plain, plain, plain,
                plain, rows(Z, Y + 1), rows(Z + 1, Y), rows(Z, Y + 1), rows(Z + 1, Y),
                rows(2, Z, 1), rows(2, 1, Y), rows(n_gy), rows(n_gz),
                dma((3, 8)), dma((3, 8)), dma((2,)), dma((2,)), dma((2, 2)), dma((2, 2)),
                dma((n_gy - 1,)), dma((n_gy - 1,)), dma((n_gz - 1,)), dma((n_gz - 1,)),
            ],
            compiler_params=pltpu.CompilerParams(
                collective_id=0, has_side_effects=True, vmem_limit_bytes=67043328
            ),
        )(*[split(block) for block in blocks])
        field = field.reshape(Z, T, Y, LANES).transpose(0, 2, 1, 3).reshape(Z, Y, X)
        return field, dt.reshape(())

    spec = P("gz", "gy", None)
    return jax.shard_map(
        shards, mesh=mesh, in_specs=(spec,) * 4, out_specs=(spec, P()), check_vma=False
    )
```

profile of v0, /device:TPU:0, one launch (start us, length us, event | category | flops | bytes accessed | tf_op | source)
XLA Modules:
  0.0 44.0 jit_solution(3165580822477702271)
XLA Ops:
  0.6 39.7 %shard_map.59 = (f32[16,64,128]{2,1,0:T(8,128)}, f32[1,1]{1,0:T(1,128)}) custom-call(f32[16,64,128]{2,1,0:T(8,128)} %bitcast.27, f32[16,64,128]{2,1,0:T(8,128)} %bitcast.28, f32[16,64,128]{2,1,0:T(8,128)} %bitcast.29, f32[16,64,128]{2,1,0:T(8,128)} %bitcast.30), custom_call_target="tpu_custom_call" | custom-call | tf_op jit(solution)/shard_map/pallas_call | solution.py:506
  40.4 1.9 %copy.8 = f32[16,8,1024]{2,1,0:T(8,128)} copy(f32[16,8,1024]{2,1,0:T(8,128)} %bitcast.26) | data formatting | bytes 1048576
where the time goes:
time: 44.8 us; the launch traced here: 44 us
  Pallas kernels  39.7 us (89%)
  between operations  2.34 us (5%)
  local copies, waits for them, and re-layouts  1.89 us (4%)
    pallas_call x1, Pallas kernels, shards(): pl.pallas_call(functools.partial(kernel, n_gy, n_gz), out_shape=(jax.Shap...  39.7 us
    unnamed x1, local copies, waits for them, and re-layouts  1.89 us

commit v1 on v0

v1 whole, which is shorter than its diff:
```python
import functools

import jax
import jax.numpy as jnp
from jax import lax
from jax.experimental import pallas as pl
from jax.experimental.pallas import tpu as pltpu
from jax.sharding import PartitionSpec as P

NEWTON = 5
LANES = 128
GROUP = 8

tilt_floor = 0.1
courant = 0.45
epsilon = 1e-06
tiny = 1e-30

MESH = pl.DeviceIdType.MESH


def lane_of(value):
    return lax.broadcasted_iota(jnp.int32, value.shape, value.ndim - 1)


def x_next(value):
    turned = pltpu.roll(value, LANES - 1, value.ndim - 1)
    carried = pltpu.roll(turned, value.shape[-2] - 1, value.ndim - 2)
    return jnp.where(lane_of(value) == LANES - 1, carried, turned)


def x_prev(value):
    turned = pltpu.roll(value, 1, value.ndim - 1)
    carried = pltpu.roll(turned, 1, value.ndim - 2)
    return jnp.where(lane_of(value) == 0, carried, turned)


def solve_offset(g, tilt_a, tilt_b, tilt_d):
    volume = jnp.clip(g, 0.0, 1.0)
    lesser = jnp.minimum(volume, 1.0 - volume)
    low = jnp.minimum(tilt_a, tilt_b)
    high = jnp.maximum(tilt_a, tilt_b)
    n1 = jnp.minimum(low, tilt_d)
    middle = jnp.maximum(low, tilt_d)
    n2 = jnp.minimum(middle, high)
    n3 = jnp.maximum(middle, high)
    summed = tilt_a + tilt_b + tilt_d
    inverse = 1.0 / jnp.maximum(n1, tiny)
    third = inverse * (1.0 / 3.0)
    product = n2 * n3
    target = 2.0 * product * lesser
    gap = jnp.maximum(n1 + n2 - n3, 0.0)
    rate = 2.0 * n2 - 0.5 * gap * (gap * inverse)
    offset = 0.5 * summed - (product - target) / rate
    for repeat in range(NEWTON - 1):
        p1 = jnp.minimum(offset, n1)
        q1 = offset - p1
        m2 = jnp.maximum(offset - n2, 0.0)
        p2 = jnp.minimum(m2, n1)
        q2 = m2 - p2
        p3 = jnp.minimum(jnp.maximum(offset - n3, 0.0), n1)
        s1, s2, s3 = p1 * p1, p2 * p2, p3 * p3
        squares = s1 - s2 - s3
        cubes = s1 * p1 - s2 * p2 - s3 * p3
        q = q1 - q2
        rate = squares * inverse + (q + q)
        volume_part = cubes * third + q * (q1 + q2 + n1)
        offset = offset - (volume_part - target) / rate
    return jnp.where(volume > 0.5, summed - offset, offset)


def face_flux(cross, offset, tilt_a, tilt_b, slope):
    turn = slope * cross
    height = jnp.abs(turn)
    reach = offset - jnp.where(turn > 0, 0.0, jnp.abs(slope) - height)

    def parts(value):
        inside = jnp.maximum(value, 0.0)
        p = jnp.minimum(inside, height)
        q = inside - p
        return p * p * p, q * (q + height)

    reach_a = reach - tilt_a
    p0, q0 = parts(reach)
    p1, q1 = parts(reach_a)
    p2, q2 = parts(reach - tilt_b)
    p3, q3 = parts(reach_a - tilt_b)
    cubes = (p0 - p1) - (p2 - p3)
    wholes = (q0 - q1) - (q2 - q3)
    combo = cubes * ((1.0 / 3.0) / jnp.maximum(height, tiny)) + wholes
    return cross * combo / (2.0 * tilt_a * tilt_b)


def kernel(
    n_gy, n_gz, f_hbm, vx_hbm, vy_hbm, vz_hbm, out_ref, dt_ref,
    f_ref, vx_ref, vy_ref, vz_ref, load_sem,
    g0, g1, g2, sx0, dx0, sx1, dx1, sx2, dx2,
    off0, ta0, tb0, sd0, off1, ta1, tb1, sd1, off2, ta2, tb2, sd2,
    vx, vy, vz, fy, fz, part_y, part_z,
    halo0_send, halo0_recv, halo1_send, halo1_recv, halo2_send, halo2_recv,
    vel_send, vel_recv, py_send, py_recv, pz_send, pz_recv,
):
    Z = f_ref.shape[0]
    T = sx0.shape[2]
    Y = f_ref.shape[1] // T
    loads = []
    for i, (source, target) in enumerate(
        ((f_hbm, f_ref), (vx_hbm, vx_ref), (vy_hbm, vy_ref), (vz_hbm, vz_ref))
    ):
        loads.append(pltpu.make_async_copy(source, target, load_sem.at[i]))
        loads[-1].start()
    my = lax.axis_index("gy")
    mz = lax.axis_index("gz")

    def at(dz, dy):
        return {
            "gy": lax.rem(my + dy + n_gy, n_gy),
            "gz": lax.rem(mz + dz + n_gz, n_gz),
        }

    barrier = pltpu.get_barrier_semaphore()
    greeted = [(0, i) for i in range(1, n_gy)] + [(i, 0) for i in range(1, n_gz)]
    greeted += [(a, b) for a in (-1, 1) for b in (-1, 1)]
    for dz, dy in greeted:
        pl.semaphore_signal(barrier, inc=1, device_id=at(dz, dy), device_id_type=MESH)

    def rows_of(ref, z, y):
        return ref[z, pl.ds(y, T, stride=Y), :]

    def gather(low, high, body, carry):
        count = high - low
        grouped = max(u for u in range(1, GROUP + 1) if count % u == 0)

        def step(i, carry):
            for u in range(grouped):
                carry = body(low + i * grouped + u, carry)
            return carry
        return lax.fori_loop(0, count // grouped, step, carry)

    def loop(low, high, body):
        def step(i, carry):
            body(i)
            return carry
        gather(low, high, step, 0)

    def halo_copies(g, spans, sends, recvs):
        copies = []
        for index, (dz, dy, src_z, dst_z, src_y, dst_y) in enumerate(spans):
            copies.append(pltpu.make_async_remote_copy(
                src_ref=g.at[src_z, src_y],
                dst_ref=g.at[dst_z, dst_y],
                send_sem=sends.at[index],
                recv_sem=recvs.at[index],
                device_id=at(dz, dy),
                device_id_type=MESH,
            ))
        return copies

    def span(side, count, pad, depth):
        if side == 0:
            return pl.ds(pad, count), pl.ds(pad, count)
        if side > 0:
            return pl.ds(pad + count - depth, depth), pl.ds(pad - depth, depth)
        return pl.ds(pad, depth), pl.ds(pad + count, depth)

    def spans_for(sides, pad_z, pad_y):
        return [
            (dz, dy, *span(dz, Z, pad_z, pad_z), *span(dy, Y, pad_y, pad_y))
            for dz, dy in sides
        ]

    Y_SIDES = [(0, -1), (0, 1)]
    Z_SIDES = [(a, b) for a in (-1, 1) for b in (0, -1, 1)]

    def fill(z, total):
        for y in range(Y):
            f = rows_of(f_ref, z, y)
            g0[z + 1, y + 1] = f
            total = total + 4.0 * f * (1.0 - f)
        return total

    loads[0].wait()
    total = gather(0, Z, fill, jnp.zeros((T, LANES), jnp.float32))

    def fill_velocity(z, peak):
        for y in range(Y):
            a = rows_of(vx_ref, z, y)
            b = rows_of(vy_ref, z, y)
            c = rows_of(vz_ref, z, y)
            vx[z, y] = a
            vy[z, y + 1] = b
            vz[z + 1, y] = c
            peak = jnp.maximum(peak, jnp.maximum(jnp.abs(a), jnp.maximum(jnp.abs(b), jnp.abs(c))))
        return peak

    for copy in loads[1:]:
        copy.wait()
    peak = gather(0, Z, fill_velocity, jnp.zeros((T, LANES), jnp.float32))
    first_row = lax.broadcasted_iota(jnp.int32, (T, LANES), 0) == 0

    def joined(sums, peaks):
        sums = jnp.broadcast_to(jnp.sum(sums, axis=0, keepdims=True), (T, LANES))
        peaks = jnp.broadcast_to(jnp.max(peaks, axis=0, keepdims=True), (T, LANES))
        return jnp.where(first_row, sums, peaks)

    def gathered(part, count):
        sums = part[0]
        peaks = part[0]
        for i in range(1, count):
            sums = sums + part[i]
            peaks = jnp.maximum(peaks, part[i])
        return jnp.where(first_row, sums, 0.0), jnp.where(first_row, 0.0, peaks)

    part_y[my] = joined(total, peak)
    pl.semaphore_wait(barrier, len(greeted))
    vel_copies = [
        pltpu.make_async_remote_copy(
            src_ref=vy.at[:, pl.ds(Y, 1)], dst_ref=vy.at[:, pl.ds(0, 1)],
            send_sem=vel_send.at[0], recv_sem=vel_recv.at[0],
            device_id=at(0, 1), device_id_type=MESH,
        ),
        pltpu.make_async_remote_copy(
            src_ref=vz.at[pl.ds(Z, 1)], dst_ref=vz.at[pl.ds(0, 1)],
            send_sem=vel_send.at[1], recv_sem=vel_recv.at[1],
            device_id=at(1, 0), device_id_type=MESH,
        ),
    ]

    def part_copies(part, mine, send, recv, count, along_y):
        copies = []
        for i in range(1, count):
            copies.append(pltpu.make_async_remote_copy(
                src_ref=part.at[mine], dst_ref=part.at[mine],
                send_sem=send.at[i - 1], recv_sem=recv.at[i - 1],
                device_id=at(0, i) if along_y else at(i, 0), device_id_type=MESH,
            ))
        return copies

    y_parts = part_copies(part_y, my, py_send, py_recv, n_gy, True)
    for copy in y_parts:
        copy.start()
    halos0 = halo_copies(g0, spans_for(Y_SIDES + Z_SIDES, 1, 1), halo0_send, halo0_recv)
    for copy in halos0:
        copy.start()
    for copy in vel_copies:
        copy.start()

    def smooth_rows(g, sx, dx, z, y, kz, ky):
        value = g[pl.ds(z, kz), pl.ds(y, ky)]
        pair = value + x_next(value)
        pair_before = x_prev(pair)
        sx[pl.ds(z, kz), pl.ds(y, ky)] = pair + pair_before
        dx[pl.ds(z, kz), pl.ds(y, ky)] = pair - pair_before

    def smooth_zero(arr):
        mid = arr[1:-1]
        return (arr[:-2] + mid) + (mid + arr[2:])

    def smooth_one(arr):
        pair = arr[:, :-1] + arr[:, 1:]
        return pair[:, :-1] + pair[:, 1:]

    def plane(refs, dim, z, y, kz, ky, parts=1):
        g, sx, dx, off, ta, tb, sd = refs
        s = sx[pl.ds(z, kz + 2), pl.ds(y, ky + 2)]
        d = dx[pl.ds(z, kz + 2), pl.ds(y, ky + 2)]
        grad_zero = smooth_one(s[2:] - s[:-2]) * (1.0 / 32.0)
        across = smooth_zero(s)
        grad_one = (across[:, 2:] - across[:, :-2]) * (1.0 / 32.0)
        grad_cells = smooth_one(smooth_zero(d)) * (1.0 / 32.0)
        slopes = (grad_zero, grad_one, grad_cells)
        low = 0
        for part in range(parts):
            count = (ky - low) // (parts - part)
            cut = [value[:, low:low + count] for value in slopes]
            slope = cut[dim]
            tilt_a, tilt_b = [jnp.abs(cut[e]) + tilt_floor for e in range(3) if e != dim]
            value = g[pl.ds(z + 1, kz), pl.ds(y + 1 + low, count)]
            where = (pl.ds(z, kz), pl.ds(y + low, count))
            off[where] = solve_offset(value, tilt_a, tilt_b, jnp.abs(slope))
            ta[where] = tilt_a
            tb[where] = tilt_b
            sd[where] = slope
            low += count

    def block(body, zs, y, ky, kz=1):
        count = len(zs) // kz
        step = zs[1] - zs[0] if len(zs) > 1 else 1
        loop(0, count, lambda i: body(zs[0] + step * kz * i, y, kz, ky))

    def planes(refs, dim, parts=1):
        return lambda z, y, kz, ky: plane(refs, dim, z, y, kz, ky, parts)

    def smooths(refs):
        return lambda z, y, kz, ky: smooth_rows(refs[0], refs[1], refs[2], z, y, kz, ky)

    own = range(0, Z)
    refs0 = (g0, sx0, dx0, off0, ta0, tb0, sd0)
    refs1 = (g1, sx1, dx1, off1, ta1, tb1, sd1)
    refs2 = (g2, sx2, dx2, off2, ta2, tb2, sd2)

    half = Z // 2
    block(smooths(refs0), range(1, Z + 1), 1, Y)
    block(planes(refs0, 2, 2), range(1, half), 1, Y - 2)
    for copy in y_parts:
        copy.wait()
    part_z[mz] = joined(*gathered(part_y, n_gy))
    z_parts = part_copies(part_z, mz, pz_send, pz_recv, n_gz, False)
    for copy in z_parts:
        copy.start()
    block(planes(refs0, 2, 2), range(half, Z - 1), 1, Y - 2)
    for copy in halos0:
        copy.wait()
    block(smooths(refs0), (0, Z + 1), 0, Y + 2)
    block(smooths(refs0), range(1, Z + 1), 0, 1)
    block(smooths(refs0), range(1, Z + 1), Y + 1, 1)
    block(planes(refs0, 2), own, 0, 1, 2)
    block(planes(refs0, 2), own, Y - 1, 1, 2)
    block(planes(refs0, 2, 2), (0, Z - 1), 1, Y - 2)

    def donors(z, y, kz, ky):
        where = (pl.ds(z, kz), pl.ds(y, ky))
        upward = vx[where] > 0
        for ref in (off0, ta0, tb0, sd0):
            value = ref[where]
            ref[where] = jnp.where(upward, value, x_next(value))

    block(donors, own, 0, Y // 2)
    block(donors, own, Y // 2, Y - Y // 2)
    for copy in z_parts:
        copy.wait()
    sums, peaks = gathered(part_z, n_gz)
    cells_all = float(Z * Y * T * LANES * n_gy * n_gz)
    share = jnp.broadcast_to(jnp.sum(sums, keepdims=True), (T, LANES)) / cells_all
    umax = jnp.broadcast_to(jnp.max(peaks, keepdims=True), (T, LANES))
    step_value = courant / ((umax + epsilon) * (1.0 + share))
    dt_ref[0, 0] = jnp.max(step_value)
    dt = step_value[None, None]

    def x_update(z, y, kz, ky):
        where = (pl.ds(z, kz), pl.ds(y, ky))
        cross = dt * vx[where]
        flux = face_flux(cross, off0[where], ta0[where], tb0[where], sd0[where])
        value = g0[pl.ds(z + 1, kz), pl.ds(y + 1, ky)]
        g1[pl.ds(z + 1, kz), pl.ds(y + 2, ky)] = (value - flux + x_prev(flux)) / (
            1.0 - cross + x_prev(cross)
        )

    deep = spans_for([(a, b) for a in (-1, 1) for b in (-1, 1)], 1, 2)
    spans1 = []
    for depth in (1, 2):
        for dy in (-1, 1):
            src, dst = span(dy, Y, 2, 2)
            near = (0, 1)[(dy > 0) == (depth == 1)]
            spans1.append((
                0, dy, pl.ds(1, Z), pl.ds(1, Z),
                pl.ds(src.start + near, 1), pl.ds(dst.start + near, 1),
            ))
    for dz in (-1, 1):
        spans1.append((dz, 0, *span(dz, Z, 1, 1), pl.ds(2, Y), pl.ds(2, Y)))
    spans1 += deep
    halos1 = halo_copies(g1, spans1, halo1_send, halo1_recv)

    block(x_update, own, 0, 1, 2)
    block(x_update, own, Y - 1, 1, 2)
    for copy in halos1[:2]:
        copy.start()
    block(x_update, own, 1, 1, 2)
    block(x_update, own, Y - 2, 1, 2)
    for copy in halos1[2:4]:
        copy.start()
    block(x_update, (0, Z - 1), 2, Y - 4)
    for copy in halos1[4:]:
        copy.start()
    block(x_update, range(1, Z - 1), 2, Y - 4)
    for copy in vel_copies:
        copy.wait()

    block(smooths(refs1), range(1, Z + 1), 2, Y)
    block(planes(refs1, 1, 2), range(1, Z - 1), 2, Y - 2)
    for copy in halos1[:2]:
        copy.wait()
    block(smooths(refs1), range(1, Z + 1), 1, 1)
    block(smooths(refs1), range(1, Z + 1), Y + 2, 1)
    block(planes(refs1, 1), range(1, Z - 1), 1, 1, 2)
    block(planes(refs1, 1), range(1, Z - 1), Y, 1, 2)
    for copy in halos1[2:]:
        copy.wait()
    block(smooths(refs1), (0, Z + 1), 0, Y + 4)
    block(smooths(refs1), range(1, Z + 1), 0, 1)
    block(smooths(refs1), range(1, Z + 1), Y + 3, 1)
    block(planes(refs1, 1, 3), (0, Z - 1), 0, Y + 2)
    block(planes(refs1, 1), range(1, Z - 1), 0, 1, 2)
    block(planes(refs1, 1), range(1, Z - 1), Y + 1, 1, 2)

    def between(refs, velocity, at_face, below, above):
        cross = dt * velocity[at_face]
        upward = cross > 0

        def donor(ref):
            return jnp.where(upward, ref[below], ref[above])

        return face_flux(cross, *[donor(ref) for ref in refs[3:]])

    def y_flux(z, y, kz, ky):
        rows = pl.ds(z, kz)
        face = (rows, pl.ds(y, ky))
        fy[face] = between(refs1, vy, face, face, (rows, pl.ds(y + 1, ky)))

    def y_update(z, y, kz, ky):
        rows = pl.ds(z, kz)
        low, high = pl.ds(y, ky), pl.ds(y + 1, ky)
        value = g1[pl.ds(z + 1, kz), pl.ds(y + 2, ky)]
        g2[pl.ds(z + 2, kz), pl.ds(y + 1, ky)] = (value - fy[rows, high] + fy[rows, low]) / (
            1.0 - dt * vy[rows, high] + dt * vy[rows, low]
        )

    halos2 = halo_copies(g2, spans_for(Y_SIDES + Z_SIDES, 2, 1), halo2_send, halo2_recv)
    block(y_flux, own, 0, 2)
    block(y_flux, own, Y - 1, 2)
    block(y_update, own, 0, 1, 2)
    block(y_update, own, Y - 1, 1, 2)
    for copy in halos2[:2]:
        copy.start()
    for zs in ((0, 1), (Z - 2, Z - 1)):
        block(y_flux, zs, 2, 2)
        block(y_flux, zs, 4, Y - 5)
        block(y_update, zs, 1, Y - 2)
    for copy in halos2[2:]:
        copy.start()
    block(y_flux, range(2, Z - 2), 2, 2)
    block(y_flux, range(2, Z - 2), 4, Y - 5)
    block(y_update, range(2, Z - 2), 1, Y - 2)

    block(smooths(refs2), range(2, Z + 2), 1, Y)
    block(planes(refs2, 0, 2), range(2, Z), 1, Y - 2)
    for copy in halos2[:2]:
        copy.wait()
    block(smooths(refs2), range(2, Z + 2), 0, 1)
    block(smooths(refs2), range(2, Z + 2), Y + 1, 1)
    block(planes(refs2, 0), range(2, Z), 0, 1, 2)
    block(planes(refs2, 0), range(2, Z), Y - 1, 1, 2)
    for copy in halos2[2:]:
        copy.wait()
    for zs in ((0, 1), (Z + 2, Z + 3)):
        block(smooths(refs2), zs, 0, Y + 2)
    for zs in ((0, 1), (Z, Z + 1)):
        block(planes(refs2, 0, 3), zs, 0, Y)

    def z_flux(z, y, kz, ky):
        face, above = (pl.ds(z, kz), pl.ds(y, ky)), (pl.ds(z + 1, kz), pl.ds(y, ky))
        fz[face] = between(refs2, vz, face, face, above)

    def z_fluxes(z):
        z_flux(z, 0, 1, Y // 2)
        z_flux(z, Y // 2, 1, Y - Y // 2)

    def z_update(z):
        for y in range(Y):
            value = (g2[z + 2, y + 1] - fz[z + 1, y] + fz[z, y]) / (
                1.0 - step_value * vz[z + 1, y] + step_value * vz[z, y]
            )
            out_ref[z, pl.ds(y, T, stride=Y), :] = value

    z_fluxes(0)
    loop(1, Z + 1, z_fluxes)
    loop(0, Z, z_update)


def writer(field_ref, step_ref, out_ref, dt_ref, sem):
    copy = pltpu.make_async_copy(field_ref, out_ref, sem)
    copy.start()
    dt_ref[0, 0] = step_ref[0, 0]
    copy.wait()


def solution(mesh):
    n_gy, n_gz = mesh.shape["gy"], mesh.shape["gz"]

    def shards(*blocks):
        Z, Y, X = blocks[0].shape
        T = X // LANES

        def split(block):
            return block.reshape(Z, Y, T, LANES).transpose(0, 2, 1, 3).reshape(Z, T * Y, LANES)

        def rows(*lead):
            return pltpu.VMEM((*lead, T, LANES), jnp.float32)

        dma = pltpu.SemaphoreType.DMA
        field, dt = pl.pallas_call(
            functools.partial(kernel, n_gy, n_gz),
            out_shape=(
                pltpu.VMEM((Z, T * Y, LANES), jnp.float32),
                pltpu.SMEM((1, 1), jnp.float32),
            ),
            in_specs=[pl.BlockSpec(memory_space=pltpu.HBM)] * 4,
            out_specs=(
                pl.BlockSpec(memory_space=pltpu.VMEM),
                pl.BlockSpec(memory_space=pltpu.SMEM),
            ),
            scratch_shapes=[
                *[pltpu.VMEM((Z, T * Y, LANES), jnp.float32)] * 4, dma((4,)),
                rows(Z + 2, Y + 2), rows(Z + 2, Y + 4), rows(Z + 4, Y + 2),
                *[rows(Z + 2, Y + 2)] * 2, *[rows(Z + 2, Y + 4)] * 2, *[rows(Z + 4, Y + 2)] * 2,
                *[rows(Z, Y)] * 4, *[rows(Z, Y + 2)] * 4, *[rows(Z + 2, Y)] * 4,
                rows(Z, Y), rows(Z, Y + 1), rows(Z + 1, Y), rows(Z, Y + 1), rows(Z + 1, Y),
                rows(n_gy), rows(n_gz),
                dma((8,)), dma((8,)), dma((10,)), dma((10,)), dma((8,)), dma((8,)),
                dma((2,)), dma((2,)),
                dma((n_gy - 1,)), dma((n_gy - 1,)), dma((n_gz - 1,)), dma((n_gz - 1,)),
            ],
            compiler_params=pltpu.CompilerParams(
                collective_id=0, has_side_effects=True, vmem_limit_bytes=66416640
            ),
        )(*[split(block) for block in blocks])
        field, dt = pl.pallas_call(
            writer,
            out_shape=(
                jax.ShapeDtypeStruct((Z, T * Y, LANES), jnp.float32),
                jax.ShapeDtypeStruct((1, 1), jnp.float32),
            ),
            in_specs=[
                pl.BlockSpec(memory_space=pltpu.VMEM),
                pl.BlockSpec(memory_space=pltpu.SMEM),
            ],
            out_specs=(
                pl.BlockSpec(memory_space=pltpu.HBM),
                pl.BlockSpec(memory_space=pltpu.SMEM),
            ),
            scratch_shapes=[dma],
        )(
            pltpu.with_memory_space_constraint(field, pltpu.VMEM),
            pltpu.with_memory_space_constraint(dt, pltpu.SMEM),
        )
        field = field.reshape(Z, T, Y, LANES).transpose(0, 2, 1, 3).reshape(Z, Y, X)
        return field, dt.reshape(())

    spec = P("gz", "gy", None)
    return jax.shard_map(
        shards, mesh=mesh, in_specs=(spec,) * 4, out_specs=(spec, P()), check_vma=False
    )
```

time: 44.8 us -> 39.8 us (0.89); the launches traced: 44 us -> 39.7 us
  local copies, waits for them, and re-layouts: 1.89 us -> 0 us
  between operations: 2.34 us -> 0.8 us
  Pallas kernels: 39.7 us -> 38.9 us
    unnamed x1 -> x0, local copies, waits for them, and re-layouts: 1.89 us -> none
    pallas_call x1 -> x2, Pallas kernels: 39.7 us -> 38.9 us  [the longest x1 37.6 us: shards(): pl.pallas_call(functools.partial(kernel, n_gy, n_gz), out_shape=(pltpu.VM...]
where the time goes in v1:
time: 39.8 us; the launch traced here: 39.7 us
  Pallas kernels  38.9 us (98%)
  between operations  0.8 us (2%)
    pallas_call x1, Pallas kernels, shards(): pl.pallas_call(functools.partial(kernel, n_gy, n_gz), out_shape=(pltpu.VM...  37.6 us
    pallas_call x1, Pallas kernels, shards(): pl.pallas_call(writer, out_shape=(jax.ShapeDtypeStruct((Z, T * Y, LANES),...  1.32 us

profile of v1, /device:TPU:0, one launch (start us, length us, event | category | flops | bytes accessed | tf_op | source)
XLA Modules:
  0.0 39.7 jit_solution(7302688059029278163)
XLA Ops:
  0.6 37.6 %shard_map.59 = (f32[16,64,128]{2,1,0:T(8,128)S(1)}, f32[1,1]{1,0:T(1,128)S(4)}) custom-call(f32[16,64,128]{2,1,0:T(8,128)} %bitcast.26, f32[16,64,128]{2,1,0:T(8,128)} %bitcast.27, f32[16,64,128]{2,1,0:T(8,128)} %bitcast.28, f32[16,64,128]{2,1,0:T(8,128)} %bitcast.29), custom_call_target="tpu_custom_call" | custom-call | tf_op jit(solution)/shard_map/pallas_call | solution.py:491
  38.2 1.3 %shard_map.60 = (f32[16,64,128]{2,1,0:T(8,128)}, f32[1,1]{1,0:T(1,128)}) custom-call(f32[16,64,128]{2,1,0:T(8,128)S(1)} %get-tuple-element.6.field_ref, f32[1,1]{1,0:T(1,128)S(4)} %get-tuple-element.7.step_ref), custom_call_target="tpu_custom_call" | custom-call | tf_op jit(solution)/shard_map/pallas_call | solution.py:517

commit v2 on v1

v2 whole, which is shorter than its diff:
```python
import functools

import jax
import jax.numpy as jnp
from jax import lax
from jax.experimental import pallas as pl
from jax.experimental.pallas import tpu as pltpu
from jax.sharding import PartitionSpec as P

NEWTON = 5
CHUNKS = 4
LANES = 128
GROUP = 8

tilt_floor = 3.2
courant = 0.45
epsilon = 1e-06
tiny = 1e-30
tiny_unit = 1e-15

MESH = pl.DeviceIdType.MESH


def lane_of(value):
    return lax.broadcasted_iota(jnp.int32, value.shape, value.ndim - 1)


def x_next(value):
    turned = pltpu.roll(value, LANES - 1, value.ndim - 1)
    carried = pltpu.roll(turned, value.shape[-2] - 1, value.ndim - 2)
    return jnp.where(lane_of(value) == LANES - 1, carried, turned)


def x_prev(value):
    turned = pltpu.roll(value, 1, value.ndim - 1)
    carried = pltpu.roll(turned, 1, value.ndim - 2)
    return jnp.where(lane_of(value) == 0, carried, turned)


def solve_offset(g, tilt_a, tilt_b, tilt_d):
    volume = jnp.clip(g, 0.0, 1.0)
    lesser = jnp.minimum(volume, 1.0 - volume)
    low = jnp.minimum(tilt_a, tilt_b)
    high = jnp.maximum(tilt_a, tilt_b)
    unit = jnp.maximum(jnp.minimum(low, tilt_d), tiny_unit)
    middle = jnp.maximum(low, tilt_d)
    inverse = 1.0 / unit
    n2 = jnp.minimum(middle, high) * inverse
    n3 = jnp.maximum(middle, high) * inverse
    above = n2 + 1.0
    summed = above + n3
    product = n2 * n3
    target = product * (lesser + lesser)
    gap = 0.5 * jnp.maximum(above - n3, 0.0)
    offset = 0.5 * (summed - (product - target) / (n2 - gap * gap))
    for repeat in range(NEWTON - 1):
        p1 = jnp.minimum(offset, 1.0)
        q1 = offset - p1
        m2 = jnp.maximum(offset - n2, 0.0)
        p2 = jnp.minimum(m2, 1.0)
        q2 = m2 - p2
        p3 = jnp.maximum(offset - n3, 0.0)
        s1, s2, s3 = p1 * p1, p2 * p2, p3 * p3
        squares = s1 - s2 - s3
        cubes = s1 * p1 - s2 * p2 - s3 * p3
        q = q1 - q2
        rate = squares + (q + q)
        volume_part = cubes * (1.0 / 3.0) + q * (q1 + (q2 + 1.0))
        offset = offset - (volume_part - target) / rate
    return jnp.where(volume > 0.5, summed - offset, offset) * unit


def face_flux(cross, offset, tilt_a, tilt_b, slope):
    turn = slope * cross
    height = jnp.abs(turn)
    reach = offset - jnp.where(turn > 0, 0.0, jnp.abs(slope) - height)

    def parts(value):
        inside = jnp.maximum(value, 0.0)
        p = jnp.minimum(inside, height)
        q = inside - p
        return p * p * p, q * (q + height)

    reach_a = reach - tilt_a
    p0, q0 = parts(reach)
    p1, q1 = parts(reach_a)
    p2, q2 = parts(reach - tilt_b)
    p3, q3 = parts(reach_a - tilt_b)
    cubes = (p0 - p1) - (p2 - p3)
    wholes = (q0 - q1) - (q2 - q3)
    combo = cubes * ((1.0 / 3.0) / jnp.maximum(height, tiny)) + wholes
    return cross * combo / (2.0 * tilt_a * tilt_b)


def between(dt, planes, velocity, at_face, below, above):
    cross = dt * velocity[at_face]
    upward = cross > 0
    donor = [jnp.where(upward, ref[below], ref[above]) for ref in planes]
    return face_flux(cross, *donor)


def kernel(
    n_gy, n_gz, f_hbm, vx_hbm, vy_hbm, vz_hbm,
    g2, fz, vz, off2, ta2, tb2, sd2, step_ref, dt_ref,
    f_ref, vx_ref, vy_ref, vz_ref, load_sem,
    g0, g1, sx0, dx0, sx1, dx1, sx2, dx2,
    off0, ta0, tb0, sd0, off1, ta1, tb1, sd1,
    vx, vy, fy, part,
    halo0_send, halo0_recv, halo1_send, halo1_recv, halo2_send, halo2_recv,
    vel_send, vel_recv, part_sem,
):
    Z = f_ref.shape[0]
    T = sx0.shape[2]
    Y = f_ref.shape[1] // T
    loads = []
    for i, (source, target) in enumerate(
        ((f_hbm, f_ref), (vx_hbm, vx_ref), (vy_hbm, vy_ref), (vz_hbm, vz_ref))
    ):
        loads.append(pltpu.make_async_copy(source, target, load_sem.at[i]))
        loads[-1].start()
    my = lax.axis_index("gy")
    mz = lax.axis_index("gz")

    def at(dz, dy):
        return {
            "gy": lax.rem(my + dy + n_gy, n_gy),
            "gz": lax.rem(mz + dz + n_gz, n_gz),
        }

    barrier = pltpu.get_barrier_semaphore()
    greeted = [(a, b) for a in range(n_gz) for b in range(n_gy)][1:]
    for dz, dy in greeted:
        pl.semaphore_signal(barrier, inc=1, device_id=at(dz, dy), device_id_type=MESH)

    def rows_of(ref, z, y):
        return ref[z, pl.ds(y, T, stride=Y), :]

    def gather(low, high, body, carry):
        count = high - low
        grouped = max(u for u in range(1, GROUP + 1) if count % u == 0)

        def step(i, carry):
            for u in range(grouped):
                carry = body(low + i * grouped + u, carry)
            return carry
        return lax.fori_loop(0, count // grouped, step, carry)

    def loop(low, high, body):
        def step(i, carry):
            body(i)
            return carry
        gather(low, high, step, 0)

    def halo_copies(g, spans, sends, recvs):
        copies = []
        for index, (dz, dy, src_z, dst_z, src_y, dst_y) in enumerate(spans):
            copies.append(pltpu.make_async_remote_copy(
                src_ref=g.at[src_z, src_y],
                dst_ref=g.at[dst_z, dst_y],
                send_sem=sends.at[index],
                recv_sem=recvs.at[index],
                device_id=at(dz, dy),
                device_id_type=MESH,
            ))
        return copies

    def span(side, count, pad, depth):
        if side == 0:
            return pl.ds(pad, count), pl.ds(pad, count)
        if side > 0:
            return pl.ds(pad + count - depth, depth), pl.ds(pad - depth, depth)
        return pl.ds(pad, depth), pl.ds(pad + count, depth)

    def spans_for(sides, pad_z, pad_y):
        return [
            (dz, dy, *span(dz, Z, pad_z, pad_z), *span(dy, Y, pad_y, pad_y))
            for dz, dy in sides
        ]

    Y_SIDES = [(0, -1), (0, 1)]
    Z_SIDES = [(a, b) for a in (-1, 1) for b in (0, -1, 1)]

    def smooth_rows(g, sx, dx, z, y, kz, ky):
        value = g[pl.ds(z, kz), pl.ds(y, ky)]
        after, before = x_next(value), x_prev(value)
        sx[pl.ds(z, kz), pl.ds(y, ky)] = before + (value + value) + after
        dx[pl.ds(z, kz), pl.ds(y, ky)] = after - before

    def smooth_zero(arr):
        mid = arr[1:-1]
        return (arr[:-2] + mid) + (mid + arr[2:])

    def smooth_one(arr):
        pair = arr[:, :-1] + arr[:, 1:]
        return pair[:, :-1] + pair[:, 1:]

    def plane(refs, dim, z, y, kz, ky, parts=1):
        g, sx, dx, off, ta, tb, sd = refs
        s = sx[pl.ds(z, kz + 2), pl.ds(y, ky + 2)]
        d = dx[pl.ds(z, kz + 2), pl.ds(y, ky + 2)]
        grad_zero = smooth_one(s[2:] - s[:-2])
        across = smooth_zero(s)
        grad_one = (across[:, 2:] - across[:, :-2])
        grad_cells = smooth_one(smooth_zero(d))
        slopes = (grad_zero, grad_one, grad_cells)
        low = 0
        for part in range(parts):
            count = (ky - low) // (parts - part)
            cut = [value[:, low:low + count] for value in slopes]
            slope = cut[dim]
            tilt_a, tilt_b = [jnp.abs(cut[e]) + tilt_floor for e in range(3) if e != dim]
            value = g[pl.ds(z + 1, kz), pl.ds(y + 1 + low, count)]
            where = (pl.ds(z, kz), pl.ds(y + low, count))
            off[where] = solve_offset(value, tilt_a, tilt_b, jnp.abs(slope))
            ta[where] = tilt_a
            tb[where] = tilt_b
            sd[where] = slope
            low += count

    def block(body, zs, y, ky, kz=1):
        count = len(zs) // kz
        step = zs[1] - zs[0] if len(zs) > 1 else 1
        loop(0, count, lambda i: body(zs[0] + step * kz * i, y, kz, ky))

    def both(body, zs, ys, kz=2):
        count = len(zs) // kz

        def step(i):
            for y in ys:
                body(zs[0] + kz * i, y, kz, 1)
        loop(0, count, step)

    def planes(refs, dim, parts=1):
        return lambda z, y, kz, ky: plane(refs, dim, z, y, kz, ky, parts)

    def smooths(refs):
        return lambda z, y, kz, ky: smooth_rows(refs[0], refs[1], refs[2], z, y, kz, ky)

    own = range(0, Z)
    refs0 = (g0, sx0, dx0, off0, ta0, tb0, sd0)
    refs1 = (g1, sx1, dx1, off1, ta1, tb1, sd1)
    refs2 = (g2, sx2, dx2, off2, ta2, tb2, sd2)

    def donors(z, y, kz, ky):
        where = (pl.ds(z, kz), pl.ds(y, ky))
        upward = vx[where] > 0
        for ref in (off0, ta0, tb0, sd0):
            value = ref[where]
            ref[where] = jnp.where(upward, value, x_next(value))

    def donors_in():
        loop(1, Z - 1, lambda z: donors(z, 1, 1, Y - 2))

    def donors_edge():
        for y in (0, Y - 1):
            block(donors, own, y, 1, 4)
        for z in (0, Z - 1):
            donors(z, 1, 1, Y - 2)

    def ghost_rows(refs, spans):
        for z, y, kz, ky in spans:
            smooth_rows(*refs[:3], z, y, kz, ky)

    def fill(z, total):
        for y in range(Y):
            f = rows_of(f_ref, z, y)
            g0[z + 1, y + 1] = f
            total = total + 4.0 * f * (1.0 - f)
        return total

    loads[0].wait()
    total = gather(0, Z, fill, jnp.zeros((T, LANES), jnp.float32))

    def fill_velocity(z, peak):
        for y in range(Y):
            a = rows_of(vx_ref, z, y)
            b = rows_of(vy_ref, z, y)
            c = rows_of(vz_ref, z, y)
            vx[z, y] = a
            vy[z, y + 1] = b
            vz[z + 1, y] = c
            peak = jnp.maximum(peak, jnp.maximum(jnp.abs(a), jnp.maximum(jnp.abs(b), jnp.abs(c))))
        return peak

    for copy in loads[1:]:
        copy.wait()
    peak = gather(0, Z, fill_velocity, jnp.zeros((T, LANES), jnp.float32))
    low_lanes = lane_of(jnp.zeros((1, LANES), jnp.float32)) < LANES // 2

    def folded(sums, peaks):
        sums = jnp.sum(sums, axis=0, keepdims=True)
        peaks = jnp.max(peaks, axis=0, keepdims=True)
        sums = sums + pltpu.roll(sums, LANES // 2, 1)
        peaks = jnp.maximum(peaks, pltpu.roll(peaks, LANES // 2, 1))
        return jnp.where(low_lanes, sums, peaks)

    me = mz * n_gy + my
    part[me] = folded(total, peak)
    pl.semaphore_wait(barrier, len(greeted))
    vel_copies = [
        pltpu.make_async_remote_copy(
            src_ref=vy.at[:, pl.ds(Y, 1)], dst_ref=vy.at[:, pl.ds(0, 1)],
            send_sem=vel_send.at[0], recv_sem=vel_recv.at[0],
            device_id=at(0, 1), device_id_type=MESH,
        ),
        pltpu.make_async_remote_copy(
            src_ref=vz.at[pl.ds(Z, 1)], dst_ref=vz.at[pl.ds(0, 1)],
            send_sem=vel_send.at[1], recv_sem=vel_recv.at[1],
            device_id=at(1, 0), device_id_type=MESH,
        ),
    ]

    part_copies = [
        pltpu.make_async_remote_copy(
            src_ref=part.at[me], dst_ref=part.at[me],
            send_sem=part_sem.at[0], recv_sem=part_sem.at[1],
            device_id=at(*away), device_id_type=MESH,
        )
        for away in greeted
    ]
    for copy in part_copies:
        copy.start()
    halos0 = halo_copies(g0, spans_for(Y_SIDES + Z_SIDES, 1, 1), halo0_send, halo0_recv)
    for copy in halos0:
        copy.start()

    block(smooths(refs0), range(1, Z + 1), 1, Y)
    block(planes(refs0, 2, 2), range(1, Z - 1), 1, Y - 2)
    donors_in()
    for copy in halos0:
        copy.wait()
    for copy in vel_copies:
        copy.start()
    ghost_rows(refs0, [
        (0, 0, 1, Y + 2), (Z + 1, 0, 1, Y + 2), (1, 0, Z, 1), (1, Y + 1, Z, 1)
    ])
    both(planes(refs0, 2), own, (0, Y - 1))
    block(planes(refs0, 2, 2), (0, Z - 1), 1, Y - 2)

    donors_edge()
    others = pl.ds(0, len(greeted))
    arrived = pltpu.make_async_remote_copy(
        src_ref=part.at[others], dst_ref=part.at[others],
        send_sem=part_sem.at[0], recv_sem=part_sem.at[1],
        device_id=at(*greeted[0]), device_id_type=MESH,
    )
    arrived.wait()
    sums = peaks = part[0]
    for i in range(1, n_gy * n_gz):
        sums = sums + part[i]
        peaks = jnp.maximum(peaks, part[i])
    sums = jnp.where(low_lanes, sums, 0.0)
    peaks = jnp.where(low_lanes, 0.0, peaks)
    cells_all = float(Z * Y * T * LANES * n_gy * n_gz)
    share = jnp.broadcast_to(jnp.sum(sums, keepdims=True), (T, LANES)) / cells_all
    umax = jnp.broadcast_to(jnp.max(peaks, keepdims=True), (T, LANES))
    step_value = courant / ((umax + epsilon) * (1.0 + share))
    dt_ref[0, 0] = jnp.max(step_value)
    step_ref[...] = step_value
    dt = step_value[None, None]

    def x_update(z, y, kz, ky):
        where = (pl.ds(z, kz), pl.ds(y, ky))
        cross = dt * vx[where]
        flux = face_flux(cross, off0[where], ta0[where], tb0[where], sd0[where])
        value = g0[pl.ds(z + 1, kz), pl.ds(y + 1, ky)]
        g1[pl.ds(z + 1, kz), pl.ds(y + 2, ky)] = (value - flux + x_prev(flux)) / (
            1.0 - cross + x_prev(cross)
        )

    def y_flux(z, y, kz, ky):
        rows = pl.ds(z, kz)
        face = (rows, pl.ds(y, ky))
        fy[face] = between(dt, refs1[3:], vy, face, face, (rows, pl.ds(y + 1, ky)))

    def y_update(z, y, kz, ky):
        rows = pl.ds(z, kz)
        low, high = pl.ds(y, ky), pl.ds(y + 1, ky)
        value = g1[pl.ds(z + 1, kz), pl.ds(y + 2, ky)]
        g2[pl.ds(z + 2, kz), pl.ds(y + 1, ky)] = (value - fy[rows, high] + fy[rows, low]) / (
            1.0 - dt * vy[rows, high] + dt * vy[rows, low]
        )

    deep = spans_for([(a, b) for a in (-1, 1) for b in (-1, 1)], 1, 2)
    spans1 = []
    for depth in (1, 2):
        for dy in (-1, 1):
            src, dst = span(dy, Y, 2, 2)
            near = (0, 1)[(dy > 0) == (depth == 1)]
            spans1.append((
                0, dy, pl.ds(1, Z), pl.ds(1, Z),
                pl.ds(src.start + near, 1), pl.ds(dst.start + near, 1),
            ))
    for dz in (-1, 1):
        spans1.append((dz, 0, *span(dz, Z, 1, 1), pl.ds(2, Y), pl.ds(2, Y)))
    spans1 += deep
    halos1 = halo_copies(g1, spans1, halo1_send, halo1_recv)

    both(x_update, own, (0, Y - 1))
    for copy in halos1[:2]:
        copy.start()
    both(x_update, own, (1, Y - 2))
    for copy in halos1[2:4]:
        copy.start()
    block(x_update, (0, Z - 1), 2, Y - 4)
    for copy in halos1[4:]:
        copy.start()
    block(x_update, range(1, Z - 1), 2, Y - 4)
    block(smooths(refs1), range(1, Z + 1), 2, Y)
    block(planes(refs1, 1, 2), range(1, Z - 1), 2, Y - 2)
    block(y_flux, range(1, Z - 1), 2, 2)
    block(y_flux, range(1, Z - 1), 4, Y - 5)
    for copy in vel_copies:
        copy.wait()
    for copy in halos1[:2]:
        copy.wait()
    ghost_rows(refs1, [(1, 1, Z, 1), (1, Y + 2, Z, 1)])
    both(planes(refs1, 1), range(1, Z - 1), (1, Y))
    for copy in halos1[2:]:
        copy.wait()
    ghost_rows(refs1, [
        (0, 0, 1, Y + 4), (Z + 1, 0, 1, Y + 4), (1, 0, Z, 1), (1, Y + 3, Z, 1)
    ])
    block(planes(refs1, 1, 3), (0, Z - 1), 0, Y + 2)
    both(planes(refs1, 1), range(1, Z - 1), (0, Y + 1))

    halos2 = halo_copies(g2, spans_for(Y_SIDES + Z_SIDES, 2, 1), halo2_send, halo2_recv)
    both_faces = lambda z, y, kz, ky: (y_flux(z, 0, kz, 2), y_flux(z, Y - 1, kz, 2))
    block(both_faces, own, 0, 2)
    both(y_update, own, (0, Y - 1))
    for copy in halos2[:2]:
        copy.start()
    block(y_flux, (0, Z - 1), 2, 2)
    block(y_flux, (0, Z - 1), 4, Y - 5)
    for zs in ((0, 1), (Z - 2, Z - 1)):
        block(y_update, zs, 1, Y - 2)
    for copy in halos2[2:]:
        copy.start()
    block(y_update, range(2, Z - 2), 1, Y - 2)

    block(smooths(refs2), range(2, Z + 2), 1, Y)
    block(planes(refs2, 0, 2), range(2, Z), 1, Y - 2)

    def z_flux(z):
        for y in (1, Y // 2):
            face, above = (pl.ds(z, 1), pl.ds(y, 3)), (pl.ds(z + 1, 1), pl.ds(y, 3))
            fz[face] = between(dt, refs2[3:], vz, face, face, above)

    loop(2, Z - 1, z_flux)
    for copy in halos2[:2]:
        copy.wait()
    ghost_rows(refs2, [(2, 0, Z, 1), (2, Y + 1, Z, 1)])
    both(planes(refs2, 0), range(2, Z), (0, Y - 1))
    for copy in halos2[2:]:
        copy.wait()
    ghost_rows(refs2, [(0, 0, 2, Y + 2), (Z + 2, 0, 2, Y + 2)])
    for zs in ((0, 1), (Z, Z + 1)):
        block(planes(refs2, 0, 3), zs, 0, Y)


def finish(
    g2, fz_in, vz, off, ta, tb, sd, step_ref, dt_in, out_hbm, dt_ref, fz, field, sems
):
    Z, Y, T = fz_in.shape[0] - 1, *fz_in.shape[1:3]
    dt_ref[0, 0] = dt_in[0, 0]
    step = step_ref[...]
    dt = step[None, None]
    per = Z // CHUNKS
    copies = []

    def flux(z, y, kz, ky):
        face, above = (pl.ds(z, kz), pl.ds(y, ky)), (pl.ds(z + 1, kz), pl.ds(y, ky))
        fz[face] = between(dt, (off, ta, tb, sd), vz, face, face, above)

    done = 0
    for chunk in range(CHUNKS):
        low, high = chunk * per, (chunk + 1) * per
        for z in range(done, high + 1):
            if 2 <= z < Z - 1:
                flux(z, 0, 1, 1)
                flux(z, Y - 1, 1, 1)
                fz[z, pl.ds(1, Y - 2)] = fz_in[z, pl.ds(1, Y - 2)]
            else:
                flux(z, 0, 1, Y // 2)
                flux(z, Y // 2, 1, Y - Y // 2)
        done = high + 1
        for z in range(low, high):
            for y in range(Y):
                value = (g2[z + 2, y + 1] - fz[z + 1, y] + fz[z, y]) / (
                    1.0 - step * vz[z + 1, y] + step * vz[z, y]
                )
                field[z, pl.ds(y, T, stride=Y), :] = value
        part = pl.ds(low, per)
        copies.append(pltpu.make_async_copy(field.at[part], out_hbm.at[part], sems.at[chunk]))
        copies[-1].start()
    for copy in copies:
        copy.wait()


def solution(mesh):
    n_gy, n_gz = mesh.shape["gy"], mesh.shape["gz"]

    def shards(*blocks):
        Z, Y, X = blocks[0].shape
        T = X // LANES

        def split(block):
            return block.reshape(Z, Y, T, LANES).transpose(0, 2, 1, 3).reshape(Z, T * Y, LANES)

        def rows(*lead):
            return pltpu.VMEM((*lead, T, LANES), jnp.float32)

        dma = pltpu.SemaphoreType.DMA
        in_vmem = pl.BlockSpec(memory_space=pltpu.VMEM)
        in_smem = pl.BlockSpec(memory_space=pltpu.SMEM)
        kept = (
            rows(Z + 4, Y + 2), rows(Z + 1, Y), rows(Z + 1, Y), *[rows(Z + 2, Y)] * 4
        )
        *state, dt = pl.pallas_call(
            functools.partial(kernel, n_gy, n_gz),
            out_shape=(
                *kept, pltpu.VMEM((T, LANES), jnp.float32), pltpu.SMEM((1, 1), jnp.float32),
            ),
            in_specs=[pl.BlockSpec(memory_space=pltpu.HBM)] * 4,
            out_specs=(*[in_vmem] * (len(kept) + 1), in_smem),
            scratch_shapes=[
                *[pltpu.VMEM((Z, T * Y, LANES), jnp.float32)] * 4, dma((4,)),
                rows(Z + 2, Y + 2), rows(Z + 2, Y + 4),
                *[rows(Z + 2, Y + 2)] * 2, *[rows(Z + 2, Y + 4)] * 2, *[rows(Z + 4, Y + 2)] * 2,
                *[rows(Z, Y)] * 4, *[rows(Z, Y + 2)] * 4,
                rows(Z, Y), rows(Z, Y + 1), rows(Z, Y + 1),
                pltpu.VMEM((n_gy * n_gz, 1, LANES), jnp.float32),
                dma((8,)), dma((8,)), dma((10,)), dma((10,)), dma((8,)), dma((8,)),
                dma((2,)), dma((2,)),
                dma((2,)),
            ],
            compiler_params=pltpu.CompilerParams(
                collective_id=0, has_side_effects=True, vmem_limit_bytes=62640128
            ),
        )(*[split(block) for block in blocks])
        field, dt = pl.pallas_call(
            finish,
            out_shape=(
                jax.ShapeDtypeStruct((Z, T * Y, LANES), jnp.float32),
                jax.ShapeDtypeStruct((1, 1), jnp.float32),
            ),
            in_specs=[*[in_vmem] * len(state), in_smem],
            out_specs=(pl.BlockSpec(memory_space=pltpu.HBM), in_smem),
            scratch_shapes=[
                rows(Z + 1, Y), pltpu.VMEM((Z, T * Y, LANES), jnp.float32), dma((CHUNKS,)),
            ],
            compiler_params=pltpu.CompilerParams(vmem_limit_bytes=16777216),
        )(
            *[pltpu.with_memory_space_constraint(value, pltpu.VMEM) for value in state],
            pltpu.with_memory_space_constraint(dt, pltpu.SMEM),
        )
        field = field.reshape(Z, T, Y, LANES).transpose(0, 2, 1, 3).reshape(Z, Y, X)
        return field, dt.reshape(())

    spec = P("gz", "gy", None)
    return jax.shard_map(
        shards, mesh=mesh, in_specs=(spec,) * 4, out_specs=(spec, P()), check_vma=False
    )
```

time: 39.8 us -> 37 us (0.930)
  Pallas kernels: 38.9 us -> 35.9 us
    pallas_call x2, Pallas kernels: 38.9 us -> 35.9 us  [the longest x1 34.1 us: shards(): pl.pallas_call(functools.partial(kernel, n_gy, n_gz), out_shape=(*kept, p...]
where the time goes in v2:
time: 37 us; the launch traced here: 36.7 us
  Pallas kernels  35.9 us (97%)
  between operations  0.8 us (2%)
    pallas_call x1, Pallas kernels, shards(): pl.pallas_call(functools.partial(kernel, n_gy, n_gz), out_shape=(*kept, p...  34.1 us
    pallas_call x1, Pallas kernels, shards(): pl.pallas_call(finish, out_shape=(jax.ShapeDtypeStruct((Z, T * Y, LANES),...  1.81 us

profile of v2, /device:TPU:0, one launch (start us, length us, event | category | flops | bytes accessed | tf_op | source)
XLA Modules:
  0.0 36.7 jit_solution(10152410790689297760)
XLA Ops:
  0.6 34.1 %shard_map.59 = (f32[20,10,8,128]{3,2,1,0:T(8,128)S(1)}, f32[17,8,8,128]{3,2,1,0:T(8,128)S(1)}, f32[17,8,8,128]{3,2,1,0:T(8,128)S(1)}, f32[18,8,8,128]{3,2,1,0:T...) custom-call(f32[16,64,128]{2,1,0:T(8,128)} %bitcast.26, ...), custom_call_target="tpu_custom_call" | custom-call | tf_op jit(solution)/shard_map/pallas_call | solution.py:519
  34.7 1.8 %shard_map.60 = (f32[16,64,128]{2,1,0:T(8,128)}, f32[1,1]{1,0:T(1,128)}) custom-call(f32[20,10,8,128]{3,2,1,0:T(8,128)S(1)} %get-tuple-element.13.g2, f32[17,8,8,128]{3,2,1,0:T(8,128)S(1)} %get-tuple-element.14.fz_in, f32[17,8,8,128]{3,2,1,0:T(8,128)S(1)} %get-tuple-element.15.vz, f32[18,8,8,128]{3,2,1,0:T(8,128)S(1)} %get-tuple-element.16.off, ...), custom_call_target="tpu_custom_call" | custom-call | tf_op jit(solution)/shard_map/pallas_call | solution.py:541

commit v3 on v2

--- a/solution.py
+++ b/solution.py
@@ -9,6 +9,7 @@
 
 NEWTON = 5
 CHUNKS = 4
+HALVES = 2
 LANES = 128
 GROUP = 8
 
@@ -101,11 +102,11 @@
 
 def kernel(
     n_gy, n_gz, f_hbm, vx_hbm, vy_hbm, vz_hbm,
-    g2, fz, vz, off2, ta2, tb2, sd2, step_ref, dt_ref,
+    middle, g2, vz, off2, ta2, tb2, sd2, step_ref, dt_ref,
     f_ref, vx_ref, vy_ref, vz_ref, load_sem,
     g0, g1, sx0, dx0, sx1, dx1, sx2, dx2,
     off0, ta0, tb0, sd0, off1, ta1, tb1, sd1,
-    vx, vy, fy, part,
+    vx, vy, fy, fz, part,
     halo0_send, halo0_recv, halo1_send, halo1_recv, halo2_send, halo2_recv,
     vel_send, vel_recv, part_sem,
 ):
@@ -135,9 +136,9 @@
     def rows_of(ref, z, y):
         return ref[z, pl.ds(y, T, stride=Y), :]
 
-    def gather(low, high, body, carry):
+    def gather(low, high, body, carry, most=GROUP):
         count = high - low
-        grouped = max(u for u in range(1, GROUP + 1) if count % u == 0)
+        grouped = max(u for u in range(1, most + 1) if count % u == 0)
 
         def step(i, carry):
             for u in range(grouped):
@@ -145,11 +146,11 @@
             return carry
         return lax.fori_loop(0, count // grouped, step, carry)
 
-    def loop(low, high, body):
+    def loop(low, high, body, most=GROUP):
         def step(i, carry):
             body(i)
             return carry
-        gather(low, high, step, 0)
+        gather(low, high, step, 0, most)
 
     def halo_copies(g, spans, sends, recvs):
         copies = []
@@ -178,7 +179,8 @@
         ]
 
     Y_SIDES = [(0, -1), (0, 1)]
-    Z_SIDES = [(a, b) for a in (-1, 1) for b in (0, -1, 1)]
+    Z_SIDES = [(-1, 0), (1, 0)]
+    CORNERS = [(a, b) for a in (-1, 1) for b in (-1, 1)]
 
     def smooth_rows(g, sx, dx, z, y, kz, ky):
         value = g[pl.ds(z, kz), pl.ds(y, ky)]
@@ -233,8 +235,8 @@
     def planes(refs, dim, parts=1):
         return lambda z, y, kz, ky: plane(refs, dim, z, y, kz, ky, parts)
 
-    def smooths(refs):
-        return lambda z, y, kz, ky: smooth_rows(refs[0], refs[1], refs[2], z, y, kz, ky)
+    def smooth_own(refs, z, y):
+        loop(z, z + Z, lambda i: smooth_rows(*refs[:3], i, y, 1, Y), Z)
 
     own = range(0, Z)
     refs0 = (g0, sx0, dx0, off0, ta0, tb0, sd0)
@@ -250,12 +252,6 @@
 
     def donors_in():
         loop(1, Z - 1, lambda z: donors(z, 1, 1, Y - 2))
-
-    def donors_edge():
-        for y in (0, Y - 1):
-            block(donors, own, y, 1, 4)
-        for z in (0, Z - 1):
-            donors(z, 1, 1, Y - 2)
 
     def ghost_rows(refs, spans):
         for z, y, kz, ky in spans:
@@ -310,6 +306,11 @@
         ),
     ]
 
+    halos0 = halo_copies(
+        g0, spans_for(Y_SIDES + Z_SIDES + CORNERS, 1, 1), halo0_send, halo0_recv
+    )
+    for copy in halos0:
+        copy.start()
     part_copies = [
         pltpu.make_async_remote_copy(
             src_ref=part.at[me], dst_ref=part.at[me],
@@ -320,24 +321,23 @@
     ]
     for copy in part_copies:
         copy.start()
-    halos0 = halo_copies(g0, spans_for(Y_SIDES + Z_SIDES, 1, 1), halo0_send, halo0_recv)
-    for copy in halos0:
-        copy.start()
-
-    block(smooths(refs0), range(1, Z + 1), 1, Y)
+
+    smooth_own(refs0, 1, 1)
     block(planes(refs0, 2, 2), range(1, Z - 1), 1, Y - 2)
     donors_in()
-    for copy in halos0:
+    for copy in halos0[2:4]:
+        copy.wait()
+    ghost_rows(refs0, [(0, 1, 1, Y), (Z + 1, 1, 1, Y)])
+    block(planes(refs0, 2, 2), (0, Z - 1), 1, Y - 2)
+    for z in (0, Z - 1):
+        donors(z, 1, 1, Y - 2)
+    for copy in halos0[:2] + halos0[4:]:
         copy.wait()
     for copy in vel_copies:
         copy.start()
-    ghost_rows(refs0, [
-        (0, 0, 1, Y + 2), (Z + 1, 0, 1, Y + 2), (1, 0, Z, 1), (1, Y + 1, Z, 1)
-    ])
+    ghost_rows(refs0, [(0, 0, Z + 2, 1), (0, Y + 1, Z + 2, 1)])
     both(planes(refs0, 2), own, (0, Y - 1))
-    block(planes(refs0, 2, 2), (0, Z - 1), 1, Y - 2)
-
-    donors_edge()
+    both(donors, own, (0, Y - 1), 4)
     others = pl.ds(0, len(greeted))
     arrived = pltpu.make_async_remote_copy(
         src_ref=part.at[others], dst_ref=part.at[others],
@@ -381,112 +381,147 @@
             1.0 - dt * vy[rows, high] + dt * vy[rows, low]
         )
 
-    deep = spans_for([(a, b) for a in (-1, 1) for b in (-1, 1)], 1, 2)
     spans1 = []
     for depth in (1, 2):
-        for dy in (-1, 1):
-            src, dst = span(dy, Y, 2, 2)
-            near = (0, 1)[(dy > 0) == (depth == 1)]
-            spans1.append((
-                0, dy, pl.ds(1, Z), pl.ds(1, Z),
-                pl.ds(src.start + near, 1), pl.ds(dst.start + near, 1),
-            ))
+        for low in range(0, Z, Z // HALVES):
+            for dy in (-1, 1):
+                src, dst = span(dy, Y, 2, 2)
+                near = (0, 1)[(dy > 0) == (depth == 1)]
+                rows = pl.ds(1 + low, Z // HALVES)
+                spans1.append((
+                    0, dy, rows, rows,
+                    pl.ds(src.start + near, 1), pl.ds(dst.start + near, 1),
+                ))
+    deep = len(spans1)
     for dz in (-1, 1):
         spans1.append((dz, 0, *span(dz, Z, 1, 1), pl.ds(2, Y), pl.ds(2, Y)))
-    spans1 += deep
+    spans1 += spans_for(CORNERS, 1, 2)
     halos1 = halo_copies(g1, spans1, halo1_send, halo1_recv)
-
-    both(x_update, own, (0, Y - 1))
-    for copy in halos1[:2]:
-        copy.start()
-    both(x_update, own, (1, Y - 2))
-    for copy in halos1[2:4]:
-        copy.start()
+    first = halos1[:deep // 2]
+    second = halos1[deep // 2:deep]
+    flat, corners = halos1[deep:deep + 2], halos1[deep + 2:]
+
+    for copies, ys in ((first, (0, Y - 1)), (second, (1, Y - 2))):
+        for part_of in range(HALVES):
+            low = part_of * (Z // HALVES)
+            both(x_update, range(low, low + Z // HALVES), ys)
+            for copy in copies[2 * part_of:2 * part_of + 2]:
+                copy.start()
     block(x_update, (0, Z - 1), 2, Y - 4)
-    for copy in halos1[4:]:
+    for copy in flat + corners:
         copy.start()
     block(x_update, range(1, Z - 1), 2, Y - 4)
-    block(smooths(refs1), range(1, Z + 1), 2, Y)
+    smooth_own(refs1, 1, 2)
     block(planes(refs1, 1, 2), range(1, Z - 1), 2, Y - 2)
-    block(y_flux, range(1, Z - 1), 2, 2)
-    block(y_flux, range(1, Z - 1), 4, Y - 5)
+    for copy in flat:
+        copy.wait()
+    ghost_rows(refs1, [(0, 2, 1, Y), (Z + 1, 2, 1, Y)])
+    block(planes(refs1, 1, 2), (0, Z - 1), 2, Y - 2)
+    block(y_flux, own, 2, 2)
+    block(y_flux, own, 4, Y - 5)
     for copy in vel_copies:
         copy.wait()
-    for copy in halos1[:2]:
+    for copy in first:
         copy.wait()
     ghost_rows(refs1, [(1, 1, Z, 1), (1, Y + 2, Z, 1)])
     both(planes(refs1, 1), range(1, Z - 1), (1, Y))
-    for copy in halos1[2:]:
+    for copy in second + corners:
         copy.wait()
     ghost_rows(refs1, [
-        (0, 0, 1, Y + 4), (Z + 1, 0, 1, Y + 4), (1, 0, Z, 1), (1, Y + 3, Z, 1)
+        (1, 0, Z, 1), (1, Y + 3, Z, 1),
+        (0, 0, 1, 2), (0, Y + 2, 1, 2), (Z + 1, 0, 1, 2), (Z + 1, Y + 2, 1, 2),
     ])
-    block(planes(refs1, 1, 3), (0, Z - 1), 0, Y + 2)
-    both(planes(refs1, 1), range(1, Z - 1), (0, Y + 1))
-
-    halos2 = halo_copies(g2, spans_for(Y_SIDES + Z_SIDES, 2, 1), halo2_send, halo2_recv)
-    both_faces = lambda z, y, kz, ky: (y_flux(z, 0, kz, 2), y_flux(z, Y - 1, kz, 2))
-    block(both_faces, own, 0, 2)
-    both(y_update, own, (0, Y - 1))
-    for copy in halos2[:2]:
-        copy.start()
-    block(y_flux, (0, Z - 1), 2, 2)
-    block(y_flux, (0, Z - 1), 4, Y - 5)
-    for zs in ((0, 1), (Z - 2, Z - 1)):
-        block(y_update, zs, 1, Y - 2)
-    for copy in halos2[2:]:
-        copy.start()
+    for z in (0, Z - 1):
+        plane(refs1, 1, z, 0, 1, 2)
+        plane(refs1, 1, z, Y, 1, 2)
+
+    per = Z // CHUNKS
+    spans2 = []
+    for low in range(0, Z, per):
+        for dy in (-1, 1):
+            rows = pl.ds(2 + low, per)
+            spans2.append((0, dy, rows, rows, *span(dy, Y, 1, 1)))
+    spans2 += spans_for(Z_SIDES + CORNERS, 2, 1)
+    halos2 = halo_copies(g2, spans2, halo2_send, halo2_recv)
+    side, flat, corners = halos2[:2 * CHUNKS], halos2[2 * CHUNKS:-4], halos2[-4:]
+
+    for chunk in (0, CHUNKS - 1, *range(1, CHUNKS - 1)):
+        low, high = chunk * per, (chunk + 1) * per
+        start, count = max(low, 1), min(high, Z - 1) - max(low, 1)
+        for y in (0, Y + 1):
+            plane(refs1, 1, start, y, count, 1)
+        for y in (0, Y - 1):
+            for z in range(low, high, 2):
+                y_flux(z, y, 2, 2)
+            y_update(low, y, per, 1)
+        for copy in side[2 * chunk:2 * chunk + 2]:
+            copy.start()
+        if chunk == CHUNKS - 1:
+            for z in (0, 1, Z - 2, Z - 1):
+                y_update(z, 1, 1, Y - 2)
+            for copy in flat + corners:
+                copy.start()
     block(y_update, range(2, Z - 2), 1, Y - 2)
 
-    block(smooths(refs2), range(2, Z + 2), 1, Y)
+    smooth_own(refs2, 2, 1)
     block(planes(refs2, 0, 2), range(2, Z), 1, Y - 2)
+    for copy in flat:
+        copy.wait()
+    ghost_rows(refs2, [(0, 1, 2, Y), (Z + 2, 1, 2, Y)])
+    for zs in ((0, 1), (Z, Z + 1)):
+        block(planes(refs2, 0, 2), zs, 1, Y - 2)
 
     def z_flux(z):
         for y in (1, Y // 2):
             face, above = (pl.ds(z, 1), pl.ds(y, 3)), (pl.ds(z + 1, 1), pl.ds(y, 3))
             fz[face] = between(dt, refs2[3:], vz, face, face, above)
 
-    loop(2, Z - 1, z_flux)
-    for copy in halos2[:2]:
-        copy.wait()
-    ghost_rows(refs2, [(2, 0, Z, 1), (2, Y + 1, Z, 1)])
-    both(planes(refs2, 0), range(2, Z), (0, Y - 1))
-    for copy in halos2[2:]:
-        copy.wait()
-    ghost_rows(refs2, [(0, 0, 2, Y + 2), (Z + 2, 0, 2, Y + 2)])
-    for zs in ((0, 1), (Z, Z + 1)):
-        block(planes(refs2, 0, 3), zs, 0, Y)
+    z_flux(0)
+    loop(1, Z + 1, z_flux)
+
+    def z_update(z):
+        for y in range(1, Y - 1):
+            value = (g2[z + 2, y + 1] - fz[z + 1, y] + fz[z, y]) / (
+                1.0 - step_value * vz[z + 1, y] + step_value * vz[z, y]
+            )
+            middle[z, pl.ds(y, T, stride=Y), :] = value
+
+    loop(0, Z, z_update)
+    for copy in side + corners:
+        copy.wait()
+    ghost_rows(refs2, [(0, 0, Z + 4, 1), (0, Y + 1, Z + 4, 1)])
+    both(planes(refs2, 0), range(0, Z + 2), (0, Y - 1), 3)
 
 
 def finish(
-    g2, fz_in, vz, off, ta, tb, sd, step_ref, dt_in, out_hbm, dt_ref, fz, field, sems
+    middle, g2, vz, off, ta, tb, sd, step_ref, dt_in, out_hbm, dt_ref, fz, field, sems
 ):
-    Z, Y, T = fz_in.shape[0] - 1, *fz_in.shape[1:3]
+    Z, T = middle.shape[0], step_ref.shape[0]
+    Y = middle.shape[1] // T
     dt_ref[0, 0] = dt_in[0, 0]
     step = step_ref[...]
     dt = step[None, None]
     per = Z // CHUNKS
     copies = []
 
-    def flux(z, y, kz, ky):
-        face, above = (pl.ds(z, kz), pl.ds(y, ky)), (pl.ds(z + 1, kz), pl.ds(y, ky))
-        fz[face] = between(dt, (off, ta, tb, sd), vz, face, face, above)
-
-    done = 0
+    def flux(z, count):
+        for side, y in enumerate((0, Y - 1)):
+            face, above = (pl.ds(z, count), pl.ds(y, 1)), (pl.ds(z + 1, count), pl.ds(y, 1))
+            fz[pl.ds(z, count), pl.ds(side, 1)] = between(
+                dt, (off, ta, tb, sd), vz, face, face, above
+            )
+
+    flux(0, 1)
     for chunk in range(CHUNKS):
         low, high = chunk * per, (chunk + 1) * per
-        for z in range(done, high + 1):
-            if 2 <= z < Z - 1:
-                flux(z, 0, 1, 1)
-                flux(z, Y - 1, 1, 1)
-                fz[z, pl.ds(1, Y - 2)] = fz_in[z, pl.ds(1, Y - 2)]
-            else:
-                flux(z, 0, 1, Y // 2)
-                flux(z, Y // 2, 1, Y - Y // 2)
-        done = high + 1
+        for z in range(low + 1, high + 1, 2):
+            flux(z, 2)
         for z in range(low, high):
-            for y in range(Y):
-                value = (g2[z + 2, y + 1] - fz[z + 1, y] + fz[z, y]) / (
+            for y in range(1, Y - 1):
+                where = pl.ds(y, T, stride=Y)
+                field[z, where, :] = middle[z, where, :]
+            for side, y in enumerate((0, Y - 1)):
+                value = (g2[z + 2, y + 1] - fz[z + 1, side] + fz[z, side]) / (
                     1.0 - step * vz[z + 1, y] + step * vz[z, y]
                 )
                 field[z, pl.ds(y, T, stride=Y), :] = value
@@ -514,7 +549,8 @@
         in_vmem = pl.BlockSpec(memory_space=pltpu.VMEM)
         in_smem = pl.BlockSpec(memory_space=pltpu.SMEM)
         kept = (
-            rows(Z + 4, Y + 2), rows(Z + 1, Y), rows(Z + 1, Y), *[rows(Z + 2, Y)] * 4
+            pltpu.VMEM((Z, T * Y, LANES), jnp.float32),
+            rows(Z + 4, Y + 2), rows(Z + 1, Y), *[rows(Z + 2, Y)] * 4,
         )
         *state, dt = pl.pallas_call(
             functools.partial(kernel, n_gy, n_gz),
@@ -528,9 +564,9 @@
                 rows(Z + 2, Y + 2), rows(Z + 2, Y + 4),
                 *[rows(Z + 2, Y + 2)] * 2, *[rows(Z + 2, Y + 4)] * 2, *[rows(Z + 4, Y + 2)] * 2,
                 *[rows(Z, Y)] * 4, *[rows(Z, Y + 2)] * 4,
-                rows(Z, Y), rows(Z, Y + 1), rows(Z, Y + 1),
+                rows(Z, Y), rows(Z, Y + 1), rows(Z, Y + 1), rows(Z + 1, Y),
                 pltpu.VMEM((n_gy * n_gz, 1, LANES), jnp.float32),
-                dma((8,)), dma((8,)), dma((10,)), dma((10,)), dma((8,)), dma((8,)),
+                dma((8,)), dma((8,)), *[dma((4 * HALVES + 6,))] * 2, *[dma((2 * CHUNKS + 6,))] * 2,
                 dma((2,)), dma((2,)),
                 dma((2,)),
             ],
@@ -547,7 +583,7 @@
             in_specs=[*[in_vmem] * len(state), in_smem],
             out_specs=(pl.BlockSpec(memory_space=pltpu.HBM), in_smem),
             scratch_shapes=[
-                rows(Z + 1, Y), pltpu.VMEM((Z, T * Y, LANES), jnp.float32), dma((CHUNKS,)),
+                rows(Z + 1, 2), pltpu.VMEM((Z, T * Y, LANES), jnp.float32), dma((CHUNKS,)),
             ],
             compiler_params=pltpu.CompilerParams(vmem_limit_bytes=16777216),
         )(

time: 37 us -> 35.7 us (0.965)
  Pallas kernels: 35.9 us -> 34.9 us
    pallas_call x1, Pallas kernels: 34.1 us -> 33.4 us  [shards(): pl.pallas_call(functools.partial(kernel, n_gy, n_gz), out_shape=(*kept, p...]
where the time goes in v3:
time: 35.7 us; the launch traced here: 35.5 us
  Pallas kernels  34.9 us (98%)
  between operations  0.64 us (2%)
    pallas_call x1, Pallas kernels, shards(): pl.pallas_call(functools.partial(kernel, n_gy, n_gz), out_shape=(*kept, p...  33.4 us
    pallas_call x1, Pallas kernels, shards(): pl.pallas_call(finish, out_shape=(jax.ShapeDtypeStruct((Z, T * Y, LANES),...  1.55 us

profile of v3, /device:TPU:0, one launch (start us, length us, event | category | flops | bytes accessed | tf_op | source)
XLA Modules:
  0.0 35.5 jit_solution(1677950208172233298)
XLA Ops:
  0.6 33.4 %shard_map.59 = (f32[16,64,128]{2,1,0:T(8,128)S(1)}, f32[20,10,8,128]{3,2,1,0:T(8,128)S(1)}, f32[17,8,8,128]{3,2,1,0:T(8,128)S(1)}, f32[18,8,8,128]{3,2,1,0:T(8,...) custom-call(f32[16,64,128]{2,1,0:T(8,128)} %bitcast.26, ...), custom_call_target="tpu_custom_call" | custom-call | tf_op jit(solution)/shard_map/pallas_call | solution.py:555
  34.0 1.6 %shard_map.60 = (f32[16,64,128]{2,1,0:T(8,128)}, f32[1,1]{1,0:T(1,128)}) custom-call(f32[16,64,128]{2,1,0:T(8,128)S(1)} %get-tuple-element.13.middle, f32[20,10,8,128]{3,2,1,0:T(8,128)S(1)} %get-tuple-element.14.g2, f32[17,8,8,128]{3,2,1,0:T(8,128)S(1)} %get-tuple-element.15.vz, f32[18,8,8,128]{3,2,1,0:T(8,128)S(1)} %get-tuple-element.16.off, ...), custom_call_target="tpu_custom_call" | custom-call | tf_op jit(solution)/shard_map/pallas_call | solution.py:577

commit v4 on v3

--- a/solution.py
+++ b/solution.py
@@ -56,18 +56,15 @@
     offset = 0.5 * (summed - (product - target) / (n2 - gap * gap))
     for repeat in range(NEWTON - 1):
         p1 = jnp.minimum(offset, 1.0)
-        q1 = offset - p1
-        m2 = jnp.maximum(offset - n2, 0.0)
-        p2 = jnp.minimum(m2, 1.0)
-        q2 = m2 - p2
+        p2 = jnp.clip(offset - n2, 0.0, 1.0)
         p3 = jnp.maximum(offset - n3, 0.0)
         s1, s2, s3 = p1 * p1, p2 * p2, p3 * p3
         squares = s1 - s2 - s3
         cubes = s1 * p1 - s2 * p2 - s3 * p3
-        q = q1 - q2
+        outer = jnp.clip(offset, 1.0, above)
+        q = outer - 1.0
         rate = squares + (q + q)
-        volume_part = cubes * (1.0 / 3.0) + q * (q1 + (q2 + 1.0))
-        offset = offset - (volume_part - target) / rate
+        offset = (offset * squares - cubes * (1.0 / 3.0) + (q * outer + target)) / rate
     return jnp.where(volume > 0.5, summed - offset, offset) * unit
 
 
@@ -100,9 +97,25 @@
     return face_flux(cross, *donor)
 
 
+def edge_flux(dt, planes, velocity, flux, low, high, y, column):
+    while low < high:
+        count = min(2, high - low)
+        face, above = (pl.ds(low, count), pl.ds(y, 1)), (pl.ds(low + 1, count), pl.ds(y, 1))
+        flux[pl.ds(low, count), pl.ds(column, 1)] = between(dt, planes, velocity, face, face, above)
+        low += count
+
+
+def edge_update(g, velocity, flux, field, step, planes, Y, y, column):
+    for z in planes:
+        value = (g[z + 2, y + 1] - flux[z + 1, column] + flux[z, column]) / (
+            1.0 - step * velocity[z + 1, y] + step * velocity[z, y]
+        )
+        field[z, pl.ds(y, value.shape[0], stride=Y), :] = value
+
+
 def kernel(
     n_gy, n_gz, f_hbm, vx_hbm, vy_hbm, vz_hbm,
-    middle, g2, vz, off2, ta2, tb2, sd2, step_ref, dt_ref,
+    middle, g2, vz, off2, ta2, tb2, sd2, step_ref,
     f_ref, vx_ref, vy_ref, vz_ref, load_sem,
     g0, g1, sx0, dx0, sx1, dx1, sx2, dx2,
     off0, ta0, tb0, sd0, off1, ta1, tb1, sd1,
@@ -129,7 +142,13 @@
         }
 
     barrier = pltpu.get_barrier_semaphore()
+    def hops(away):
+        steps = (away[0] // 2, away[1] // 4, away[1] % 4)
+        return sum(min(step, 4 - step) for step in steps)
+
     greeted = [(a, b) for a in range(n_gz) for b in range(n_gy)][1:]
+    greeted.sort(key=hops, reverse=True)
+    far = sum(hops(away) >= 4 for away in greeted)
     for dz, dy in greeted:
         pl.semaphore_signal(barrier, inc=1, device_id=at(dz, dy), device_id_type=MESH)
 
@@ -309,8 +328,6 @@
     halos0 = halo_copies(
         g0, spans_for(Y_SIDES + Z_SIDES + CORNERS, 1, 1), halo0_send, halo0_recv
     )
-    for copy in halos0:
-        copy.start()
     part_copies = [
         pltpu.make_async_remote_copy(
             src_ref=part.at[me], dst_ref=part.at[me],
@@ -319,12 +336,14 @@
         )
         for away in greeted
     ]
-    for copy in part_copies:
+    for copy in part_copies[:far] + halos0 + part_copies[far:]:
         copy.start()
 
     smooth_own(refs0, 1, 1)
     block(planes(refs0, 2, 2), range(1, Z - 1), 1, Y - 2)
     donors_in()
+    for copy in vel_copies:
+        copy.start()
     for copy in halos0[2:4]:
         copy.wait()
     ghost_rows(refs0, [(0, 1, 1, Y), (Z + 1, 1, 1, Y)])
@@ -333,8 +352,6 @@
         donors(z, 1, 1, Y - 2)
     for copy in halos0[:2] + halos0[4:]:
         copy.wait()
-    for copy in vel_copies:
-        copy.start()
     ghost_rows(refs0, [(0, 0, Z + 2, 1), (0, Y + 1, Z + 2, 1)])
     both(planes(refs0, 2), own, (0, Y - 1))
     both(donors, own, (0, Y - 1), 4)
@@ -355,7 +372,6 @@
     share = jnp.broadcast_to(jnp.sum(sums, keepdims=True), (T, LANES)) / cells_all
     umax = jnp.broadcast_to(jnp.max(peaks, keepdims=True), (T, LANES))
     step_value = courant / ((umax + epsilon) * (1.0 + share))
-    dt_ref[0, 0] = jnp.max(step_value)
     step_ref[...] = step_value
     dt = step_value[None, None]
 
@@ -381,13 +397,15 @@
             1.0 - dt * vy[rows, high] + dt * vy[rows, low]
         )
 
+    middle_row = Z // 2 + 1
+    halves = ((0, middle_row), (middle_row, Z))
     spans1 = []
     for depth in (1, 2):
-        for low in range(0, Z, Z // HALVES):
+        for low, high in halves:
             for dy in (-1, 1):
                 src, dst = span(dy, Y, 2, 2)
                 near = (0, 1)[(dy > 0) == (depth == 1)]
-                rows = pl.ds(1 + low, Z // HALVES)
+                rows = pl.ds(1 + low, high - low)
                 spans1.append((
                     0, dy, rows, rows,
                     pl.ds(src.start + near, 1), pl.ds(dst.start + near, 1),
@@ -399,21 +417,20 @@
     halos1 = halo_copies(g1, spans1, halo1_send, halo1_recv)
     first = halos1[:deep // 2]
     second = halos1[deep // 2:deep]
-    flat, corners = halos1[deep:deep + 2], halos1[deep + 2:]
+    flat1, corners1 = halos1[deep:deep + 2], halos1[deep + 2:]
 
     for copies, ys in ((first, (0, Y - 1)), (second, (1, Y - 2))):
-        for part_of in range(HALVES):
-            low = part_of * (Z // HALVES)
-            both(x_update, range(low, low + Z // HALVES), ys)
-            for copy in copies[2 * part_of:2 * part_of + 2]:
+        for at_half, (low, high) in enumerate(halves):
+            both(x_update, range(low, high), ys, 3 if (high - low) % 3 == 0 else 1)
+            for copy in copies[2 * at_half:2 * at_half + 2]:
                 copy.start()
     block(x_update, (0, Z - 1), 2, Y - 4)
-    for copy in flat + corners:
+    for copy in flat1 + corners1:
         copy.start()
     block(x_update, range(1, Z - 1), 2, Y - 4)
     smooth_own(refs1, 1, 2)
     block(planes(refs1, 1, 2), range(1, Z - 1), 2, Y - 2)
-    for copy in flat:
+    for copy in flat1:
         copy.wait()
     ghost_rows(refs1, [(0, 2, 1, Y), (Z + 1, 2, 1, Y)])
     block(planes(refs1, 1, 2), (0, Z - 1), 2, Y - 2)
@@ -421,19 +438,11 @@
     block(y_flux, own, 4, Y - 5)
     for copy in vel_copies:
         copy.wait()
-    for copy in first:
-        copy.wait()
-    ghost_rows(refs1, [(1, 1, Z, 1), (1, Y + 2, Z, 1)])
-    both(planes(refs1, 1), range(1, Z - 1), (1, Y))
-    for copy in second + corners:
-        copy.wait()
-    ghost_rows(refs1, [
-        (1, 0, Z, 1), (1, Y + 3, Z, 1),
-        (0, 0, 1, 2), (0, Y + 2, 1, 2), (Z + 1, 0, 1, 2), (Z + 1, Y + 2, 1, 2),
-    ])
-    for z in (0, Z - 1):
-        plane(refs1, 1, z, 0, 1, 2)
-        plane(refs1, 1, z, Y, 1, 2)
+    for at_half, (low, high) in enumerate(halves):
+        for copy in first[2 * at_half:2 * at_half + 2]:
+            copy.wait()
+        ghost_rows(refs1, [(1 + low, y, high - low, 1) for y in (1, Y + 2)])
+        both(planes(refs1, 1), range(max(low - 1, 1), high - 1), (1, Y), 1)
 
     per = Z // CHUNKS
     spans2 = []
@@ -445,7 +454,7 @@
     halos2 = halo_copies(g2, spans2, halo2_send, halo2_recv)
     side, flat, corners = halos2[:2 * CHUNKS], halos2[2 * CHUNKS:-4], halos2[-4:]
 
-    for chunk in (0, CHUNKS - 1, *range(1, CHUNKS - 1)):
+    def chunk_out(chunk):
         low, high = chunk * per, (chunk + 1) * per
         start, count = max(low, 1), min(high, Z - 1) - max(low, 1)
         for y in (0, Y + 1):
@@ -456,11 +465,22 @@
             y_update(low, y, per, 1)
         for copy in side[2 * chunk:2 * chunk + 2]:
             copy.start()
-        if chunk == CHUNKS - 1:
-            for z in (0, 1, Z - 2, Z - 1):
-                y_update(z, 1, 1, Y - 2)
-            for copy in flat + corners:
-                copy.start()
+
+    for at_half, (low, high) in enumerate(halves):
+        for copy in second[2 * at_half:2 * at_half + 2] + corners1[2 - 2 * at_half:4 - 2 * at_half]:
+            copy.wait()
+        end = at_half * (Z - 1)
+        ghost = at_half * (Z + 1)
+        ghost_rows(refs1, [(1 + low, y, high - low, 1) for y in (0, Y + 3)])
+        ghost_rows(refs1, [(ghost, 0, 1, 2), (ghost, Y + 2, 1, 2)])
+        for y in (0, Y):
+            plane(refs1, 1, end, y, 1, 2)
+        chunk_out(at_half * (CHUNKS - 1))
+        for z in (end, end + 1 - 2 * at_half):
+            y_update(z, 1, 1, Y - 2)
+        for copy in [flat[at_half]] + corners[2 * at_half:2 * at_half + 2]:
+            copy.start()
+        chunk_out(1 + at_half)
     block(y_update, range(2, Z - 2), 1, Y - 2)
 
     smooth_own(refs2, 2, 1)
@@ -487,46 +507,45 @@
             middle[z, pl.ds(y, T, stride=Y), :] = value
 
     loop(0, Z, z_update)
-    for copy in side + corners:
-        copy.wait()
-    ghost_rows(refs2, [(0, 0, Z + 4, 1), (0, Y + 1, Z + 4, 1)])
-    both(planes(refs2, 0), range(0, Z + 2), (0, Y - 1), 3)
+    for copy in side[:4] + corners[2:]:
+        copy.wait()
+    first_rows = 2 + Z // 2
+    ghost_rows(refs2, [(0, y, first_rows, 1) for y in (0, Y + 1)])
+    both(planes(refs2, 0), range(0, first_rows - 2), (0, Y - 1))
+    for y in (0, Y - 1):
+        edge_flux(dt, refs2[3:], vz, fz, 0, per + 1, y, y)
+        edge_update(g2, vz, fz, middle, step_value, range(0, per), Y, y, y)
+    for copy in side[4:] + corners[:2]:
+        copy.wait()
+    ghost_rows(refs2, [(first_rows, y, Z + 4 - first_rows, 1) for y in (0, Y + 1)])
+    both(planes(refs2, 0), range(first_rows - 2, Z + 2), (0, Y - 1))
 
 
 def finish(
-    middle, g2, vz, off, ta, tb, sd, step_ref, dt_in, out_hbm, dt_ref, fz, field, sems
+    middle, g2, vz, off, ta, tb, sd, step_ref, out_hbm, dt_hbm, fz, field, one, sems
 ):
     Z, T = middle.shape[0], step_ref.shape[0]
     Y = middle.shape[1] // T
-    dt_ref[0, 0] = dt_in[0, 0]
     step = step_ref[...]
+    one[...] = step[:1, :1]
+    copies = [pltpu.make_async_copy(one, dt_hbm, sems.at[CHUNKS])]
+    copies[0].start()
     dt = step[None, None]
     per = Z // CHUNKS
-    copies = []
-
-    def flux(z, count):
-        for side, y in enumerate((0, Y - 1)):
-            face, above = (pl.ds(z, count), pl.ds(y, 1)), (pl.ds(z + 1, count), pl.ds(y, 1))
-            fz[pl.ds(z, count), pl.ds(side, 1)] = between(
-                dt, (off, ta, tb, sd), vz, face, face, above
-            )
-
-    flux(0, 1)
     for chunk in range(CHUNKS):
         low, high = chunk * per, (chunk + 1) * per
-        for z in range(low + 1, high + 1, 2):
-            flux(z, 2)
-        for z in range(low, high):
-            for y in range(1, Y - 1):
-                where = pl.ds(y, T, stride=Y)
-                field[z, where, :] = middle[z, where, :]
+        if chunk > 0:
             for side, y in enumerate((0, Y - 1)):
-                value = (g2[z + 2, y + 1] - fz[z + 1, side] + fz[z, side]) / (
-                    1.0 - step * vz[z + 1, y] + step * vz[z, y]
-                )
-                field[z, pl.ds(y, T, stride=Y), :] = value
+                new = low if chunk == 1 else low + 1
+                edge_flux(dt, (off, ta, tb, sd), vz, fz, new, high + 1, y, side)
+                edge_update(g2, vz, fz, field, step, range(low, high), Y, y, side)
+            for z in range(low, high):
+                for y in range(1, Y - 1):
+                    where = pl.ds(y, T, stride=Y)
+                    field[z, where, :] = middle[z, where, :]
         part = pl.ds(low, per)
-        copies.append(pltpu.make_async_copy(field.at[part], out_hbm.at[part], sems.at[chunk]))
+        source = field if chunk > 0 else middle
+        copies.append(pltpu.make_async_copy(source.at[part], out_hbm.at[part], sems.at[chunk]))
         copies[-1].start()
     for copy in copies:
         copy.wait()
@@ -547,18 +566,17 @@
 
         dma = pltpu.SemaphoreType.DMA
         in_vmem = pl.BlockSpec(memory_space=pltpu.VMEM)
-        in_smem = pl.BlockSpec(memory_space=pltpu.SMEM)
         kept = (
             pltpu.VMEM((Z, T * Y, LANES), jnp.float32),
             rows(Z + 4, Y + 2), rows(Z + 1, Y), *[rows(Z + 2, Y)] * 4,
         )
-        *state, dt = pl.pallas_call(
+        state = pl.pallas_call(
             functools.partial(kernel, n_gy, n_gz),
             out_shape=(
-                *kept, pltpu.VMEM((T, LANES), jnp.float32), pltpu.SMEM((1, 1), jnp.float32),
+                *kept, pltpu.VMEM((T, LANES), jnp.float32),
             ),
             in_specs=[pl.BlockSpec(memory_space=pltpu.HBM)] * 4,
-            out_specs=(*[in_vmem] * (len(kept) + 1), in_smem),
+            out_specs=(in_vmem,) * (len(kept) + 1),
             scratch_shapes=[
                 *[pltpu.VMEM((Z, T * Y, LANES), jnp.float32)] * 4, dma((4,)),
                 rows(Z + 2, Y + 2), rows(Z + 2, Y + 4),
@@ -580,15 +598,15 @@
                 jax.ShapeDtypeStruct((Z, T * Y, LANES), jnp.float32),
                 jax.ShapeDtypeStruct((1, 1), jnp.float32),
             ),
-            in_specs=[*[in_vmem] * len(state), in_smem],
-            out_specs=(pl.BlockSpec(memory_space=pltpu.HBM), in_smem),
+            in_specs=[in_vmem] * len(state),
+            out_specs=(pl.BlockSpec(memory_space=pltpu.HBM),) * 2,
             scratch_shapes=[
-                rows(Z + 1, 2), pltpu.VMEM((Z, T * Y, LANES), jnp.float32), dma((CHUNKS,)),
+                rows(Z + 1, 2), pltpu.VMEM((Z, T * Y, LANES), jnp.float32),
+                pltpu.VMEM((1, 1), jnp.float32), dma((CHUNKS + 1,)),
             ],
             compiler_params=pltpu.CompilerParams(vmem_limit_bytes=16777216),
         )(
             *[pltpu.with_memory_space_constraint(value, pltpu.VMEM) for value in state],
-            pltpu.with_memory_space_constraint(dt, pltpu.SMEM),
         )
         field = field.reshape(Z, T, Y, LANES).transpose(0, 2, 1, 3).reshape(Z, Y, X)
         return field, dt.reshape(())

time: 35.7 us -> 35 us (0.980)
  Pallas kernels: 34.9 us -> 34.2 us
    pallas_call x1, Pallas kernels: 1.55 us -> 0.99 us  [shards(): pl.pallas_call(finish, out_shape=(jax.ShapeDtypeStruct((Z, T * Y, LANES),...]
where the time goes in v4:
time: 35 us; the launch traced here: 34.9 us
  Pallas kernels  34.2 us (98%)
  between operations  0.64 us (2%)
    pallas_call x1, Pallas kernels, shards(): pl.pallas_call(functools.partial(kernel, n_gy, n_gz), out_shape=(*kept, p...  33.2 us
    pallas_call x1, Pallas kernels, shards(): pl.pallas_call(finish, out_shape=(jax.ShapeDtypeStruct((Z, T * Y, LANES),...  0.99 us

profile of v4, /device:TPU:0, one launch (start us, length us, event | category | flops | bytes accessed | tf_op | source)
XLA Modules:
  0.0 34.9 jit_solution(1420397018189572432)
XLA Ops:
  0.6 33.2 %shard_map.59 = (f32[16,64,128]{2,1,0:T(8,128)S(1)}, f32[20,10,8,128]{3,2,1,0:T(8,128)S(1)}, f32[17,8,8,128]{3,2,1,0:T(8,128)S(1)}, f32[18,8,8,128]{3,2,1,0:T(8,...) custom-call(f32[16,64,128]{2,1,0:T(8,128)} %bitcast.26, ...), custom_call_target="tpu_custom_call" | custom-call | tf_op jit(solution)/shard_map/pallas_call | solution.py:573
  33.9 1.0 %shard_map.60 = (f32[16,64,128]{2,1,0:T(8,128)}, f32[1,1]{1,0:T(1,128)}) custom-call(f32[16,64,128]{2,1,0:T(8,128)S(1)} %get-tuple-element.12.middle, f32[20,10,8,128]{3,2,1,0:T(8,128)S(1)} %get-tuple-element.13.g2, f32[17,8,8,128]{3,2,1,0:T(8,128)S(1)} %get-tuple-element.14.vz, f32[18,8,8,128]{3,2,1,0:T(8,128)S(1)} %get-tuple-element.15.off, ...), custom_call_target="tpu_custom_call" | custom-call | tf_op jit(solution)/shard_map/pallas_call | solution.py:595

commit v5 on v4

--- a/solution.py
+++ b/solution.py
@@ -336,7 +336,7 @@
         )
         for away in greeted
     ]
-    for copy in part_copies[:far] + halos0 + part_copies[far:]:
+    for copy in halos0[4:] + halos0[2:4] + part_copies[:far] + halos0[:2] + part_copies[far:]:
         copy.start()
 
     smooth_own(refs0, 1, 1)
@@ -362,10 +362,18 @@
         device_id=at(*greeted[0]), device_id_type=MESH,
     )
     arrived.wait()
-    sums = peaks = part[0]
-    for i in range(1, n_gy * n_gz):
-        sums = sums + part[i]
-        peaks = jnp.maximum(peaks, part[i])
+    sums = [part[i] for i in range(GROUP)]
+    peaks = list(sums)
+    for i in range(len(sums), n_gy * n_gz):
+        at_row = i % len(sums)
+        row = part[i]
+        sums[at_row] = sums[at_row] + row
+        peaks[at_row] = jnp.maximum(peaks[at_row], row)
+    while len(sums) > 1:
+        count = len(sums) // 2
+        sums = [sums[i] + sums[i + count] for i in range(count)]
+        peaks = [jnp.maximum(peaks[i], peaks[i + count]) for i in range(count)]
+    sums, peaks = sums[0], peaks[0]
     sums = jnp.where(low_lanes, sums, 0.0)
     peaks = jnp.where(low_lanes, 0.0, peaks)
     cells_all = float(Z * Y * T * LANES * n_gy * n_gz)
@@ -419,14 +427,16 @@
     second = halos1[deep // 2:deep]
     flat1, corners1 = halos1[deep:deep + 2], halos1[deep + 2:]
 
+    for z in (0, Z - 1):
+        for y in range(0, Y, Y // 2):
+            x_update(z, y, 1, Y // 2)
+    for copy in corners1 + flat1:
+        copy.start()
     for copies, ys in ((first, (0, Y - 1)), (second, (1, Y - 2))):
         for at_half, (low, high) in enumerate(halves):
-            both(x_update, range(low, high), ys, 3 if (high - low) % 3 == 0 else 1)
+            both(x_update, range(max(low, 1), min(high, Z - 1)), ys)
             for copy in copies[2 * at_half:2 * at_half + 2]:
                 copy.start()
-    block(x_update, (0, Z - 1), 2, Y - 4)
-    for copy in flat1 + corners1:
-        copy.start()
     block(x_update, range(1, Z - 1), 2, Y - 4)
     smooth_own(refs1, 1, 2)
     block(planes(refs1, 1, 2), range(1, Z - 1), 2, Y - 2)
@@ -463,8 +473,6 @@
             for z in range(low, high, 2):
                 y_flux(z, y, 2, 2)
             y_update(low, y, per, 1)
-        for copy in side[2 * chunk:2 * chunk + 2]:
-            copy.start()
 
     for at_half, (low, high) in enumerate(halves):
         for copy in second[2 * at_half:2 * at_half + 2] + corners1[2 - 2 * at_half:4 - 2 * at_half]:
@@ -478,9 +486,15 @@
         chunk_out(at_half * (CHUNKS - 1))
         for z in (end, end + 1 - 2 * at_half):
             y_update(z, 1, 1, Y - 2)
-        for copy in [flat[at_half]] + corners[2 * at_half:2 * at_half + 2]:
+        chunk = at_half * (CHUNKS - 1)
+        for copy in (
+            corners[2 * at_half:2 * at_half + 2] + [flat[at_half]]
+            + side[2 * chunk:2 * chunk + 2]
+        ):
             copy.start()
         chunk_out(1 + at_half)
+        for copy in side[2 + 2 * at_half:4 + 2 * at_half]:
+            copy.start()
     block(y_update, range(2, Z - 2), 1, Y - 2)
 
     smooth_own(refs2, 2, 1)

time: 35 us -> 33.1 us (0.946); the launches traced: 34.9 us -> 32.6 us
  Pallas kernels: 34.2 us -> 32 us
    pallas_call x1, Pallas kernels: 33.2 us -> 31 us  [shards(): pl.pallas_call(functools.partial(kernel, n_gy, n_gz), out_shape=(*kept, p...]
where the time goes in v5:
time: 33.1 us; the launch traced here: 32.6 us
  Pallas kernels  32 us (97%)
  between operations  0.64 us (2%)
    pallas_call x1, Pallas kernels, shards(): pl.pallas_call(functools.partial(kernel, n_gy, n_gz), out_shape=(*kept, p...  31 us
    pallas_call x1, Pallas kernels, shards(): pl.pallas_call(finish, out_shape=(jax.ShapeDtypeStruct((Z, T * Y, LANES),...  0.99 us

profile of v5, /device:TPU:0, one launch (start us, length us, event | category | flops | bytes accessed | tf_op | source)
XLA Modules:
  0.0 32.6 jit_solution(15181639401017002876)
XLA Ops:
  0.6 31.0 %shard_map.59 = (f32[16,64,128]{2,1,0:T(8,128)S(1)}, f32[20,10,8,128]{3,2,1,0:T(8,128)S(1)}, f32[17,8,8,128]{3,2,1,0:T(8,128)S(1)}, f32[18,8,8,128]{3,2,1,0:T(8,...) custom-call(f32[16,64,128]{2,1,0:T(8,128)} %bitcast.26, ...), custom_call_target="tpu_custom_call" | custom-call | tf_op jit(solution)/shard_map/pallas_call | solution.py:587
  31.6 1.0 %shard_map.60 = (f32[16,64,128]{2,1,0:T(8,128)}, f32[1,1]{1,0:T(1,128)}) custom-call(f32[16,64,128]{2,1,0:T(8,128)S(1)} %get-tuple-element.12.middle, f32[20,10,8,128]{3,2,1,0:T(8,128)S(1)} %get-tuple-element.13.g2, f32[17,8,8,128]{3,2,1,0:T(8,128)S(1)} %get-tuple-element.14.vz, f32[18,8,8,128]{3,2,1,0:T(8,128)S(1)} %get-tuple-element.15.off, ...), custom_call_target="tpu_custom_call" | custom-call | tf_op jit(solution)/shard_map/pallas_call | solution.py:609

commit v6 on v5

--- a/solution.py
+++ b/solution.py
@@ -148,7 +148,7 @@
 
     greeted = [(a, b) for a in range(n_gz) for b in range(n_gy)][1:]
     greeted.sort(key=hops, reverse=True)
-    far = sum(hops(away) >= 4 for away in greeted)
+    far = sum(hops(away) >= 5 for away in greeted)
     for dz, dy in greeted:
         pl.semaphore_signal(barrier, inc=1, device_id=at(dz, dy), device_id_type=MESH)
 

time: 33.1 us -> 33 us (level)
  no operation moved by 1% of the time
where the time goes in v6:
time: 33 us; the launch traced here: 32.6 us
  Pallas kernels  32 us (97%)
  between operations  0.64 us (2%)
    pallas_call x1, Pallas kernels, shards(): pl.pallas_call(functools.partial(kernel, n_gy, n_gz), out_shape=(*kept, p...  31 us
    pallas_call x1, Pallas kernels, shards(): pl.pallas_call(finish, out_shape=(jax.ShapeDtypeStruct((Z, T * Y, LANES),...  0.99 us

profile of v6, /device:TPU:0, one launch (start us, length us, event | category | flops | bytes accessed | tf_op | source)
XLA Modules:
  0.0 32.6 jit_solution(13219563880215642708)
XLA Ops:
  0.6 31.0 %shard_map.59 = (f32[16,64,128]{2,1,0:T(8,128)S(1)}, f32[20,10,8,128]{3,2,1,0:T(8,128)S(1)}, f32[17,8,8,128]{3,2,1,0:T(8,128)S(1)}, f32[18,8,8,128]{3,2,1,0:T(8,...) custom-call(f32[16,64,128]{2,1,0:T(8,128)} %bitcast.26, ...), custom_call_target="tpu_custom_call" | custom-call | tf_op jit(solution)/shard_map/pallas_call | solution.py:587
  31.7 1.0 %shard_map.60 = (f32[16,64,128]{2,1,0:T(8,128)}, f32[1,1]{1,0:T(1,128)}) custom-call(f32[16,64,128]{2,1,0:T(8,128)S(1)} %get-tuple-element.12.middle, f32[20,10,8,128]{3,2,1,0:T(8,128)S(1)} %get-tuple-element.13.g2, f32[17,8,8,128]{3,2,1,0:T(8,128)S(1)} %get-tuple-element.14.vz, f32[18,8,8,128]{3,2,1,0:T(8,128)S(1)} %get-tuple-element.15.off, ...), custom_call_target="tpu_custom_call" | custom-call | tf_op jit(solution)/shard_map/pallas_call | solution.py:609
